TPU v7x, 32 devices: a whole 2x2x4 slice. The times are simulated.
32 devices in a mesh: dp: 8 (over z, y), tensor: 4 (over x, core).
Axes of the slice: x: 2, y: 2, z: 4, core: 2. Of those that a mesh axis runs over, the one named last changes fastest.
Arguments:
- attention: bfloat16 [4096, 4096], P('dp', 'tensor'), may hold values from -0.44921875 to 0.546875
- cotangent: bfloat16 [4096, 2048], P('dp', 'tensor'), may hold values from -0.5 to 1.5
- projection: bfloat16 [4096, 2048], P(None, 'tensor'), may hold values from -0.125 to 0.125
Outputs:
- input_grad: bfloat16 [4096, 4096], P('dp', 'tensor')
- combined: float32 [4096, 2048], P(None, 'tensor')
All inputs are finite; a program needn't handle non-finite values.
Results may differ from a plain program's by a relative error of at most 0.0004.
Values may be sent and summed in bfloat16 or wider, within the bound.
No kernel may reach another device: no remote copies, remote signals or barrier semaphores. Data moves between devices by JAX's collectives and lax.ppermute only.
A program may use at most 64 MiB of HBM per device.

v0:
```python
import functools

import jax
import jax.numpy as jnp
from jax import lax
from jax.experimental import pallas as pl
from jax.experimental.pallas import tpu as pltpu
from jax.sharding import PartitionSpec as P


epsilon = 1e-06
tiny = 1e-30
peak = 16384.0
lanes = 128


def pair_weights(low_sq, high_sq, cross):
    low_sq = jnp.maximum(low_sq, 0.0)
    high_sq = jnp.maximum(high_sq, 0.0)
    most = jnp.sqrt(low_sq) * jnp.sqrt(high_sq)
    cross = jnp.minimum(jnp.maximum(cross, -most), most)
    return 1.0 - cross / (2.0 * (low_sq + epsilon)), 1.0 - cross / (2.0 * (high_sq + epsilon))


def merge_coefs(products):
    count = len(products)
    members = [{i: None} for i in range(count)]
    table = products
    while len(table) > 1:
        half = len(table) // 2
        weights = [
            pair_weights(table[2 * i][2 * i], table[2 * i + 1][2 * i + 1], table[2 * i][2 * i + 1])
            for i in range(half)
        ]
        members = [
            {
                r: weights[i][side] if w is None else weights[i][side] * w
                for side in (0, 1)
                for r, w in members[2 * i + side].items()
            }
            for i in range(half)
        ]
        table = [
            [
                sum(
                    weights[i][a] * weights[j][b] * table[min(2 * i + a, 2 * j + b)][max(2 * i + a, 2 * j + b)]
                    for a in (0, 1)
                    for b in (0, 1)
                )
                if j >= i
                else None
                for j in range(half)
            ]
            for i in range(half)
        ]
    return [members[0][r] for r in range(count)]


def own_input_grad(cotangent, projection):
    own_rows = lax.all_to_all(projection, "tensor", split_axis=0, concat_axis=1, tiled=True)
    return lax.dot_general(
        lax.all_gather(cotangent, "tensor", axis=1, tiled=True),
        own_rows,
        (((1,), (1,)), ((), ())),
        preferred_element_type=jnp.float32,
    ).astype(jnp.bfloat16)


def whole_gathers(attention, cotangent, projection):
    n, groups = lax.axis_size("dp"), lax.axis_size("tensor")
    rows = attention.shape[0]
    input_grad = own_input_grad(cotangent, projection)
    acts = lax.all_to_all(attention, "dp", split_axis=1, concat_axis=0, tiled=True)
    acts = lax.all_gather(acts, "tensor", axis=1, tiled=True)
    cots = lax.all_gather(cotangent, "dp", axis=0, tiled=True)
    features, columns = acts.shape[1], cots.shape[1]
    grads = lax.dot_general(
        acts.reshape(n, rows, features),
        cots.reshape(n, rows, columns),
        (((1,), (1,)), ((0,), (0,))),
        preferred_element_type=jnp.float32,
    )
    gram = jnp.stack([jnp.sum(grads * grads[i], (1, 2)) for i in range(n)])
    gram = lax.psum(gram, ("dp", "tensor"))
    coefs = jnp.stack(merge_coefs([[gram[i, j] for j in range(n)] for i in range(n)]))
    bound = jnp.maximum(jnp.sum(jnp.abs(coefs) * jnp.sqrt(jnp.diagonal(gram))), tiny)
    piece = jnp.sum(coefs[:, None, None] * grads, 0)
    sent = (piece * (peak / bound)).astype(jnp.float16)
    gathered = lax.all_gather(sent, "dp", axis=0).astype(jnp.float32) * (bound / peak)
    gathered = gathered.reshape(n, groups, features // groups, columns)
    return (input_grad, gathered.transpose(1, 0, 2, 3).reshape(-1, columns))


def fetch(pairs, sems):
    copies = [pltpu.make_async_copy(source, target, sems.at[i]) for i, (source, target) in enumerate(pairs)]
    for copy in copies:
        copy.start()
    return copies


def grads_kernel(replicas, groups, before, index_ref, *refs):
    slices, refs = refs[:groups], refs[groups:]
    cots, refs = refs[:replicas], refs[replicas:]
    earlier, refs = refs[: before // replicas], refs[before // replicas :]
    grads_ref, gram_ref, acts, cotangents, held, sems = refs
    width, columns = acts.shape[3], cotangents.shape[2]
    lines = len(earlier)
    features = groups * width
    loads = fetch(
        [(slices[m], acts.at[m]) for m in range(groups)]
        + [(cots[l], cotangents.at[l]) for l in range(replicas)]
        + [(earlier[i], held.at[i]) for i in range(lines)],
        sems,
    )
    for copy in loads[: groups + replicas]:
        copy.wait()
    for l in range(replicas):
        for m in range(groups):
            at = pl.multiple_of(index_ref[m] * width, width)
            held[lines, l, pl.ds(at, width), :] = lax.dot_general(
                acts[m, l],
                cotangents[l],
                (((0,), (0,)), ((), ())),
                preferred_element_type=jnp.float32,
            )
    store = pltpu.make_async_copy(held.at[lines], grads_ref, sems.at[len(loads)])
    store.start()
    for copy in loads[groups + replicas :]:
        copy.wait()
    blocks = [(i, l) for i in range(lines + 1) for l in range(replicas)]
    pairs = [(a, b) for b in range(before, before + replicas) for a in range(b + 1)]

    def body(chunk, sums):
        at = pl.multiple_of(chunk * 8, 8)
        values = [held[i, l, pl.ds(at, 8), :] for i, l in blocks]
        fresh = []
        for (a, b), total in zip(pairs, sums):
            product = values[a] * values[b]
            for j in range(columns // lanes):
                total = total + product[:, j * lanes : (j + 1) * lanes]
            fresh.append(total)
        return tuple(fresh)

    zero = jnp.zeros((8, lanes), jnp.float32)
    sums = lax.fori_loop(0, features // 8, body, tuple(zero for _ in pairs))
    row = lax.broadcasted_iota(jnp.int32, (8, lanes), 0)
    col = lax.broadcasted_iota(jnp.int32, (8, lanes), 1)
    gram = zero
    for (a, b), total in zip(pairs, sums):
        value = jnp.sum(jnp.sum(total, axis=0, keepdims=True), axis=1, keepdims=True)
        low = jnp.minimum(index_ref[groups + a], index_ref[groups + b])
        high = jnp.maximum(index_ref[groups + a], index_ref[groups + b])
        gram = gram + jnp.where((row == low) & (col == high), value, 0.0)
    gram_ref[...] = gram
    store.wait()


def combine_kernel(replicas, groups, index_ref, gram_ref, *refs):
    blocks, (piece_ref, scale_ref, held, sems) = refs[:-4], refs[-4:]
    count = len(blocks) * replicas
    loads = fetch([(block, held.at[i]) for i, block in enumerate(blocks)], sems)
    gram = jnp.sum(gram_ref[...], axis=0)
    row = lax.broadcasted_iota(jnp.int32, gram.shape, 0)
    col = lax.broadcasted_iota(jnp.int32, gram.shape, 1)

    def entry(i, j):
        found = jnp.where((row == i) & (col == j), gram, 0.0)
        return jnp.sum(jnp.sum(found, axis=0, keepdims=True), axis=1, keepdims=True)

    products = [[entry(i, j) if j >= i else None for j in range(count)] for i in range(count)]
    coefs = merge_coefs(products)
    bound = sum(jnp.abs(coefs[i]) * jnp.sqrt(products[i][i]) for i in range(count))
    bound = jnp.maximum(bound, tiny)
    scale_ref[...] = bound * (1.0 / peak)
    weights = []
    for at in range(count):
        weight = sum(jnp.where(index_ref[groups + at] == i, coefs[i], 0.0) for i in range(count))
        weights.append(weight * (peak / bound))
    features, _ = piece_ref.shape
    for copy in loads:
        copy.wait()

    def body(chunk, carry):
        at = pl.multiple_of(chunk * 16, 16)
        total = None
        for block in range(len(blocks)):
            for l in range(replicas):
                term = held[block, l, pl.ds(at, 16), :] * weights[block * replicas + l]
                total = term if total is None else total + term
        piece_ref[pl.ds(at, 16), :] = total
        return carry

    lax.fori_loop(0, features // 16, body, 0)


def pack_kernel(index_ref, attention_ref, packed_ref):
    packed_ref[...] = attention_ref[...].reshape(packed_ref.shape)


def pack(index, attention, width):
    rows = attention.shape[0]
    return pl.pallas_call(
        pack_kernel,
        grid_spec=pltpu.PrefetchScalarGridSpec(
            num_scalar_prefetch=1,
            grid=(index.shape[0],),
            in_specs=[pl.BlockSpec((rows, width), lambda i, index: (0, index[i]))],
            out_specs=pl.BlockSpec((1, rows, width), lambda i, index: (i, 0, 0)),
        ),
        out_shape=jax.ShapeDtypeStruct((index.shape[0], rows, width), attention.dtype),
        compiler_params=pltpu.CompilerParams(vmem_limit_bytes=4 * 2**20),
        name="pack",
    )(index, attention)


def after(value, *others):
    return lax.optimization_barrier((value, *others))[0]


def unwritten(shape):
    return pl.pallas_call(
        lambda out_ref: None,
        out_shape=jax.ShapeDtypeStruct(shape, jnp.float32),
        out_specs=pl.BlockSpec(memory_space=pltpu.HBM),
        name="unwritten",
    )()


def exchanges(attention, cotangent, projection):
    n, groups = lax.axis_size("dp"), lax.axis_size("tensor")
    inner = 2 ** ((n.bit_length() - 1) // 2)
    outer, pairs = n // inner, groups // 2
    rows, features_here = attention.shape
    columns = cotangent.shape[1]
    width = features_here // n
    features = width * groups
    me, part = lax.axis_index("dp"), lax.axis_index("tensor")
    z, y = me // inner, me % inner
    x, core = part // 2, part % 2

    def along_z(value, k):
        ring = [(i * inner + j, (i + k) % outer * inner + j) for i in range(outer) for j in range(inner)]
        return lax.ppermute(value, "dp", ring)

    def along_y(value, l):
        ring = [(i * inner + j, i * inner + (j + l) % inner) for i in range(outer) for j in range(inner)]
        return lax.ppermute(value, "dp", ring)

    def along_tensor(value, j, flip):
        ring = [(a * 2 + c, (a + j) % pairs * 2 + (c ^ flip)) for a in range(pairs) for c in range(2)]
        return lax.ppermute(value, "tensor", ring)

    right = outer // 2
    arrival = [0, 1]
    for k in range(1, right + 1):
        arrival += [outer - k] if outer - k > right else []
        arrival += [k + 1] if k < right else []

    def gather_lines(value):
        found = {0: value}
        for k in arrival[1:]:
            source, step = (found[(k + 1) % outer], -1) if k > right else (found[k - 1], 1)
            found[k] = along_z(source, step)
        return {k: [found[k]] + [along_y(found[k], l) for l in range(1, inner)] for k in arrival}

    def replica_of(k, l):
        return (z - k) % outer * inner + (y - l) % inner

    cots = gather_lines(cotangent)

    own_rows = projection.reshape(groups, -1, columns)

    def rows_for(j, flip):
        target = (x + j) % pairs * 2 + (core ^ flip)
        return lax.dynamic_index_in_dim(own_rows, target, 0, keepdims=False)

    row_blocks = {
        (j, flip): along_tensor(rows_for(j, flip), j, flip) if j or flip else rows_for(0, 0)
        for j in range(pairs)
        for flip in (0, 1)
    }
    cot_blocks = {(j, 0): along_tensor(cotangent, j, 0) if j else cotangent for j in range(pairs)}
    cot_blocks.update({(j, 1): along_tensor(cot_blocks[j, 0], 0, 1) for j in range(pairs)})

    targets = [
        jnp.stack([(z + k) % outer * inner + (y + l) % inner for k in range(outer)]).astype(jnp.int32)
        for l in range(inner)
    ]
    from_y = [
        along_y(pack(targets[l], attention, width), l) if l else pack(targets[0], attention, width)
        for l in range(inner)
    ]
    slices, slots = {}, []
    for k in arrival:
        held = jnp.stack([from_y[l][k] for l in range(inner)])
        if k:
            held = along_z(held, k)
        shifted = [held] + [along_tensor(held, j, 0) for j in range(1, pairs)]
        slices[k] = shifted + [along_tensor(value, 0, 1) for value in shifted]
    for flip in (0, 1):
        slots += [(x - j) % pairs * 2 + (core ^ flip) for j in range(pairs)]

    order = [replica_of(k, l) for k in arrival for l in range(inner)]
    index = jnp.stack([jnp.asarray(v, jnp.int32) for v in slots + order])
    grads, gram = [], None
    smem, hbm = pl.BlockSpec(memory_space=pltpu.SMEM), pl.BlockSpec(memory_space=pltpu.HBM)
    for at, k in enumerate(arrival):
        operands = [*slices[k], *cots[k], *grads]
        block, partial = pl.pallas_call(
            functools.partial(grads_kernel, inner, groups, at * inner),
            in_specs=[smem] + [hbm] * len(operands),
            out_specs=(hbm, pl.BlockSpec(memory_space=pltpu.VMEM)),
            out_shape=(
                jax.ShapeDtypeStruct((inner, features, columns), jnp.float32),
                jax.ShapeDtypeStruct((8, lanes), jnp.float32),
            ),
            scratch_shapes=[
                pltpu.VMEM((groups, inner, rows, width), attention.dtype),
                pltpu.VMEM((inner, rows, columns), cotangent.dtype),
                pltpu.VMEM((at + 1, inner, features, columns), jnp.float32),
                pltpu.SemaphoreType.DMA((len(operands) + 1,)),
            ],
            cost_estimate=pl.CostEstimate(
                flops=2 * inner * rows * features * columns,
                bytes_accessed=8 * inner * features * columns,
                transcendentals=0,
            ),
        )(index, *operands)
        grads.append(block)
        gram = partial if gram is None else gram + partial

    shared = lax.all_to_all(
        jnp.broadcast_to(gram[None], (n * groups, 8, lanes)), ("dp", "tensor"), 0, 0, tiled=True
    ).reshape(n * groups, 8, lanes)
    sent, scale = pl.pallas_call(
        functools.partial(combine_kernel, inner, groups),
        in_specs=[smem, pl.BlockSpec(memory_space=pltpu.VMEM)] + [hbm] * outer,
        out_specs=(pl.BlockSpec(memory_space=pltpu.VMEM), pl.BlockSpec(memory_space=pltpu.VMEM)),
        out_shape=(
            jax.ShapeDtypeStruct((features, columns), jnp.float32),
            jax.ShapeDtypeStruct((1, 1), jnp.float32),
        ),
        scratch_shapes=[
            pltpu.VMEM((outer, inner, features, columns), jnp.float32),
            pltpu.SemaphoreType.DMA((outer,)),
        ],
        cost_estimate=pl.CostEstimate(
            flops=2 * n * features * columns, bytes_accessed=4 * n * features * columns, transcendentals=0
        ),
        name="combine",
    )(index, shared, *grads)
    combined = unwritten((groups, n, width, columns))
    lines = gather_lines(after(sent.astype(jnp.float16)))
    for l in range(inner):
        for k in arrival:
            values = lines[k][l].reshape(groups, 1, width, columns).astype(jnp.float32) * scale[0, 0]
            combined = lax.dynamic_update_slice_in_dim(combined, values, replica_of(k, l), 1)
    combined = combined.reshape(groups * n * width, columns)

    total = None
    for key in [(0, 0), (0, 1)] + [(j, flip) for j in range(1, pairs) for flip in (0, 1)]:
        theirs = cot_blocks[key]
        if key != (0, 0):
            theirs = after(theirs, lines[outer - 1 if key[0] else 1][0])
        term = lax.dot_general(theirs, row_blocks[key], (((1,), (1,)), ((), ())), preferred_element_type=jnp.float32)
        total = term if total is None else total + term
    return (total.astype(jnp.bfloat16), combined)


def on_device(attention, cotangent, projection):
    n, groups = lax.axis_size("dp"), lax.axis_size("tensor")
    aligned = (attention.shape[1] // n) % lanes == 0 and cotangent.shape[1] % lanes == 0
    if aligned and groups % 2 == 0 and 4 <= n <= 8:
        return exchanges(attention, cotangent, projection)
    return whole_gathers(attention, cotangent, projection)


def solution(mesh):
    return jax.shard_map(
        on_device,
        mesh=mesh,
        in_specs=(P("dp", "tensor"), P("dp", "tensor"), P(None, "tensor")),
        out_specs=(P("dp", "tensor"), P(None, "tensor")),
        check_vma=False,
    )
```

profile of v0, /device:TPU:0, one launch (start us, length us, event | category | flops | bytes accessed | tf_op | source)
XLA Modules:
  0.0 223.7 jit_solution(3529570945576237304)
XLA Ops:
  0.8 1.2 copy-done
  2.0 0.8 pack.3
  2.9 3.1 %collective-permute-start.1 = (bf16[4,512,128]{2,1,0:T(8,128)(2,1)S(1)}, bf16[4,512,128]{2,1,0:T(8,128)(2,1)S(1)}, u32[]{:S(2)}, u32[]{:S(2)}) collective-permute-start(bf16[4,512,128]{2,1,0:T(8,128)(2,1)S(1)} %pack.3), channel_id=1, source_target_pairs={{0,4},{4,0},{8,12},{12,8},{16,20},{20,16},{24,28},{28,24},{1,5},{5... | collective-permute-start | bytes 1572872 | tf_op jit(solution)/shard_map/ppermute | solution.py:247
  6.0 2.0 collective-permute-start.10
  8.0 2.0 collective-permute-start.16
  10.1 1.2 copy-done.1
  11.3 0.8 pack.2
  12.2 6.5 %collective-permute-done.1 = bf16[4,512,128]{2,1,0:T(8,128)(2,1)S(1)} collective-permute-done((bf16[4,512,128]{2,1,0:T(8,128)(2,1)S(1)}, bf16[4,512,128]{2,1,0:T(8,128)(2,1)S(1)}, u32[]{:S(2)}, u32[]{:S(2)}) %collective-permute-start.1) | collective-permute-done | bytes 524320 | tf_op jit(solution)/shard_map/ppermute | solution.py:247
  18.8 2.1 collective-permute-start.2
  20.9 8.2 %collective-permute-done.5.refs_5_ = bf16[512,512]{1,0:T(8,128)(2,1)S(1)} collective-permute-done((bf16[512,512]{1,0:T(8,128)(2,1)}, bf16[512,512]{1,0:T(8,128)(2,1)S(1)}, u32[]{:S(2)}, u32[]{:S(2)}) %collective-permute-start.5) | collective-permute-done | bytes 524320 | tf_op jit(solution)/shard_map/ppermute | solution.py:247
  29.1 1.8 collective-permute-start.6
  31.0 3.7 %collective-permute-start.12 = (bf16[2,512,128]{2,1,0:T(8,128)(2,1)S(1)}, bf16[2,512,128]{2,1,0:T(8,128)(2,1)S(1)}, u32[]{:S(2)}, u32[]{:S(2)}) collective-permute-start(bf16[2,512,128]{2,1,0:T(8,128)(2,1)S(1)} %pad_maximum_fusion.2), channel_id=1, source_target_pairs={{0,24},{4,28},{8,0},{12,4},{16,8},{20,12},{24,16},{28,20},{1,25},{... | collective-permute-start | bytes 786440 | tf_op jit(solution)/shard_map/ppermute | solution.py:243
  34.7 1.6 collective-permute-start.11
  36.3 0.7 copy-done.15
  37.0 3.1 %collective-permute-done.6.refs_0_ = bf16[2,512,128]{2,1,0:T(8,128)(2,1)S(1)} collective-permute-done((bf16[2,512,128]{2,1,0:T(8,128)(2,1)S(1)}, bf16[2,512,128]{2,1,0:T(8,128)(2,1)S(1)}, u32[]{:S(2)}, u32[]{:S(2)}) %collective-permute-start.6) | collective-permute-done | bytes 262176 | tf_op jit(solution)/shard_map/ppermute | solution.py:243
  40.1 9.9 %collective-permute-start.22 = (bf16[512,512]{1,0:T(8,128)(2,1)S(1)}, bf16[512,512]{1,0:T(8,128)(2,1)S(1)}, u32[]{:S(2)}, u32[]{:S(2)}) collective-permute-start(bf16[512,512]{1,0:T(8,128)(2,1)S(1)} %collective-permute-done.10.refs_4_), channel_id=1, source_target_pairs={{0,8},{4,12},{8,16},{12,20},{16,24},{20,28},{24,0},{28,4},{1,9},{5... | collective-permute-start | bytes 1572872 | tf_op jit(solution)/shard_map/ppermute | solution.py:243
  50.0 1.5 collective-permute-start.7
  51.5 15.2 %collective-permute-done.18.refs_0_ = bf16[2,512,128]{2,1,0:T(8,128)(2,1)S(1)} collective-permute-done((bf16[2,512,128]{2,1,0:T(8,128)(2,1)S(1)}, bf16[2,512,128]{2,1,0:T(8,128)(2,1)S(1)}, u32[]{:S(2)}, u32[]{:S(2)}) %collective-permute-start.18) | collective-permute-done | bytes 262176 | tf_op jit(solution)/shard_map/ppermute | solution.py:243
  66.7 1.6 collective-permute-start.13
  68.4 1.5 collective-permute-start.17
  69.9 1.3 collective-permute-start.19
  71.2 4.8 %collective-permute-done.13.refs_1_ = bf16[2,512,128]{2,1,0:T(8,128)(2,1)} collective-permute-done((bf16[2,512,128]{2,1,0:T(8,128)(2,1)S(1)}, bf16[2,512,128]{2,1,0:T(8,128)(2,1)}, u32[]{:S(2)}, u32[]{:S(2)}) %collective-permute-start.13) | collective-permute-done | bytes 262176 | tf_op jit(solution)/shard_map/ppermute | solution.py:251
  76.0 1.6 collective-permute-start.23
  77.8 3.3 %collective-permute-done.19.refs_1_ = bf16[2,512,128]{2,1,0:T(8,128)(2,1)} collective-permute-done((bf16[2,512,128]{2,1,0:T(8,128)(2,1)S(1)}, bf16[2,512,128]{2,1,0:T(8,128)(2,1)}, u32[]{:S(2)}, u32[]{:S(2)}) %collective-permute-start.19) | collective-permute-done | bytes 262176 | tf_op jit(solution)/shard_map/ppermute | solution.py:251
  83.0 4.9 %shard_map.50 = (f32[2,512,512]{2,1,0:T(8,128)}, f32[8,128]{1,0:T(8,128)}) custom-call(s32[12]{0:T(128)} %stack.91.index_ref, bf16[2,512,128]{2,1,0:T(8,128)(2,1)} %copy-done.5, bf16[2,512,128]{2,1,0:T(8,128)(2,1)} %copy-done.14, bf16[2,512,128]{2,1,0:T(8,128)(2,1)} %copy-done.15, bf16[2,512,128]{2,1,0:T(8,128)(2,1)} %copy-done.18, ...), custom_call_target="tpu_custom_call" | custom-call | flops 536870912 | bytes 4194304 | tf_op jit(solution)/shard_map/pallas_call | solution.py:309
  87.9 4.9 %shard_map.51 = (f32[2,512,512]{2,1,0:T(8,128)}, f32[8,128]{1,0:T(8,128)}) custom-call(s32[12]{0:T(128)} %stack.91.index_ref, bf16[2,512,128]{2,1,0:T(8,128)(2,1)} %copy-done.16, bf16[2,512,128]{2,1,0:T(8,128)(2,1)} %copy-done.19, bf16[2,512,128]{2,1,0:T(8,128)(2,1)} %copy-done.20, bf16[2,512,128]{2,1,0:T(8,128)(2,1)} %copy-done.22, ...), custom_call_target="tpu_custom_call" | custom-call | flops 536870912 | bytes 4194304 | tf_op jit(solution)/shard_map/pallas_call | solution.py:309
  92.9 5.8 %shard_map.52 = (f32[2,512,512]{2,1,0:T(8,128)}, f32[8,128]{1,0:T(8,128)}) custom-call(s32[12]{0:T(128)} %stack.91.index_ref, bf16[2,512,128]{2,1,0:T(8,128)(2,1)} %copy-done.17, bf16[2,512,128]{2,1,0:T(8,128)(2,1)} %collective-permute-done.13.refs_1_, bf16[2,512,128]{2,1,0:T(8,128)(2,1)} %copy-done.21, ...), custom_call_target="tpu_custom_call" | custom-call | flops 536870912 | bytes 4194304 | tf_op jit(solution)/shard_map/pallas_call | solution.py:309
  98.7 7.0 %shard_map.53 = (f32[2,512,512]{2,1,0:T(8,128)}, f32[8,128]{1,0:T(8,128)}) custom-call(s32[12]{0:T(128)} %stack.91.index_ref, bf16[2,512,128]{2,1,0:T(8,128)(2,1)} %copy-done.13, bf16[2,512,128]{2,1,0:T(8,128)(2,1)} %collective-permute-done.19.refs_1_, bf16[2,512,128]{2,1,0:T(8,128)(2,1)} %collective-permute-done.20.refs_2_, ...), custom_call_target="tpu_custom_call" | custom-call | flops 536870912 | bytes 4194304 | tf_op jit(solution)/shard_map/pallas_call | solution.py:309
  107.2 2.8 %all-to-all-start = ((f32[32,8,128]{2,1,0:T(8,128)}), f32[32,8,128]{2,1,0:T(8,128)S(1)}, u32[]{:S(2)}, u32[]{:S(2)}) async-start(f32[32,8,128]{2,1,0:T(8,128)} %broadcast_in_dim.2), calls=%async_computation | async-start | bytes 262144 | tf_op jit(solution)/shard_map/all_to_all | solution.py:332
  110.3 1.6 collective-permute-start.26
  111.9 6.3 %all-to-all-done.gram_ref = f32[32,8,128]{2,1,0:T(8,128)S(1)} async-done(((f32[32,8,128]{2,1,0:T(8,128)}), f32[32,8,128]{2,1,0:T(8,128)S(1)}, u32[]{:S(2)}, u32[]{:S(2)}) %all-to-all-start) | async-done | bytes 131104 | tf_op jit(solution)/shard_map/all_to_all | solution.py:332
  118.9 6.1 %combine.1 = (f32[512,512]{1,0:T(8,128)}, f32[1,1]{1,0:T(1,128)}) custom-call(s32[12]{0:T(128)} %stack.91.index_ref, f32[32,8,128]{2,1,0:T(8,128)} %copy-done.6, f32[2,512,512]{2,1,0:T(8,128)} %get-tuple-element.16.refs_6_.refs_0_, f32[2,512,512]{2,1,0:T(8,128)} %get-tuple-element.18.refs_7_.refs_1_, f32[2,512,512]{2,1,0:T(8,128)} %get-tuple-element.20.refs_8_.refs_2_, ...), custom_call_target="tpu_custom_call" | custom-call | flops 4194304 | bytes 8388608 | tf_op jit(solution)/shard_map/combine/pallas_call | solution.py:335
  125.0 2.1 convert_element_type.102
  127.9 3.6 %dynamic-slice_bitcast_fusion.2 = (bf16[1024,512]{1,0:T(8,128)(2,1)}, bf16[1024,512]{1,0:T(8,128)(2,1)}, bf16[1024,512]{1,0:T(8,128)(2,1)}) fusion(bf16[4,1024,512]{2,1,0:T(8,128)(2,1)} %bitcast.63, s32[]{:T(128)S(6)} %select_n.210, s32[]{:T(128)S(6)} %select_n.213, s32[]{:T(128)S(6)} %select_n.212), kind=kLoop, calls=%fused_computation.16 | loop fusion | bytes 6291468 | tf_op jit(solution)/shard_map/jit(dynamic_index_in_dim)/squeeze | solution.py:275
  131.6 1.7 collective-permute-start.30
  133.6 9.6 %collective-permute-done.24 = f16[512,512]{1,0:T(8,128)(2,1)S(1)} collective-permute-done((f16[512,512]{1,0:T(8,128)(2,1)}, f16[512,512]{1,0:T(8,128)(2,1)S(1)}, u32[]{:S(2)}, u32[]{:S(2)}) %collective-permute-start.24) | collective-permute-done | bytes 524320 | tf_op jit(solution)/shard_map/ppermute | solution.py:243
  143.2 0.8 copy-done.12
  144.0 2.0 fusion.3
  146.0 1.8 convert_multiply_fusion.7
  147.9 1.0 constant_dynamic-update-slice_fusion.7
  148.9 8.5 %collective-permute-done.27 = f16[512,512]{1,0:T(8,128)(2,1)} collective-permute-done((f16[512,512]{1,0:T(8,128)(2,1)}, f16[512,512]{1,0:T(8,128)(2,1)}, u32[]{:S(2)}, u32[]{:S(2)}) %collective-permute-start.27) | collective-permute-done | bytes 524320 | tf_op jit(solution)/shard_map/ppermute | solution.py:243
  157.6 2.0 fusion.9
  159.5 2.0 fusion.10
  161.5 17.8 %collective-permute-done.30 = bf16[1024,512]{1,0:T(8,128)(2,1)} collective-permute-done((bf16[1024,512]{1,0:T(8,128)(2,1)}, bf16[1024,512]{1,0:T(8,128)(2,1)}, u32[]{:S(2)}, u32[]{:S(2)}) %collective-permute-start.30) | collective-permute-done | bytes 1048608 | tf_op jit(solution)/shard_map/ppermute | solution.py:251
  179.4 2.2 fusion.2
  181.6 1.3 copy.8
  182.9 1.8 convert_multiply_fusion.6
  185.9 1.4 collective-permute-start.34
  187.4 1.8 convert_multiply_fusion.5
  189.2 1.0 constant_dynamic-update-slice_fusion.6
  190.2 1.0 constant_dynamic-update-slice_fusion.5
  191.2 1.8 convert_multiply_fusion.3
  193.0 7.8 %collective-permute-done.31 = f16[512,512]{1,0:T(8,128)(2,1)S(1)} collective-permute-done((f16[512,512]{1,0:T(8,128)(2,1)}, f16[512,512]{1,0:T(8,128)(2,1)S(1)}, u32[]{:S(2)}, u32[]{:S(2)}) %collective-permute-start.31) | collective-permute-done | bytes 524320 | tf_op jit(solution)/shard_map/ppermute | solution.py:243
  201.4 0.7 convert_multiply_fusion.4
  202.2 1.0 constant_dynamic-update-slice_fusion.4
  203.2 1.0 constant_dynamic-update-slice_fusion.3
  204.3 0.8 convert_multiply_fusion.2
  205.0 1.0 constant_dynamic-update-slice_fusion.2
  206.1 5.5 %collective-permute-done.34 = f16[512,512]{1,0:T(8,128)(2,1)S(1)} collective-permute-done((f16[512,512]{1,0:T(8,128)(2,1)}, f16[512,512]{1,0:T(8,128)(2,1)S(1)}, u32[]{:S(2)}, u32[]{:S(2)}) %collective-permute-start.34) | collective-permute-done | bytes 524320 | tf_op jit(solution)/shard_map/ppermute | solution.py:247
  211.6 0.8 convert_multiply_fusion.1
  212.3 1.0 constant_dynamic-update-slice_fusion.1
  213.4 8.5 %collective-permute-done.35 = f16[512,512]{1,0:T(8,128)(2,1)S(1)} collective-permute-done((f16[512,512]{1,0:T(8,128)(2,1)S(1)}, f16[512,512]{1,0:T(8,128)(2,1)S(1)}, u32[]{:S(2)}, u32[]{:S(2)}) %collective-permute-start.35) | collective-permute-done | bytes 524320 | tf_op jit(solution)/shard_map/ppermute | solution.py:247
  221.9 0.8 convert_multiply_fusion
  222.6 1.0 constant_dynamic-update-slice_fusion
  (103 shorter events, 8.1 us)
Async XLA Ops:
  0.8 1.2 copy-start
  2.9 15.8 %collective-permute-start.1 = (bf16[4,512,128]{2,1,0:T(8,128)(2,1)S(1)}, bf16[4,512,128]{2,1,0:T(8,128)(2,1)S(1)}, u32[]{:S(2)}, u32[]{:S(2)}) collective-permute-start(bf16[4,512,128]{2,1,0:T(8,128)(2,1)S(1)} %pack.3), channel_id=1, source_target_pairs={{0,4},{4,0},{8,12},{12,8},{16,20},{20,16},{24,28},{28,24},{1,5},{5... | collective-permute-start | bytes 1572872 | tf_op jit(solution)/shard_map/ppermute | solution.py:247
  6.0 23.2 %collective-permute-start.5 = (bf16[512,512]{1,0:T(8,128)(2,1)}, bf16[512,512]{1,0:T(8,128)(2,1)S(1)}, u32[]{:S(2)}, u32[]{:S(2)}) collective-permute-start(bf16[512,512]{1,0:T(8,128)(2,1)} %refs_4_.1), channel_id=1, source_target_pairs={{0,4},{4,0},{8,12},{12,8},{16,20},{20,16},{24,28},{28,24},{1,5},{5... | collective-permute-start | bytes 1572872 | tf_op jit(solution)/shard_map/ppermute | solution.py:247
  6.0 24.9 %collective-permute-start.10 = (bf16[512,512]{1,0:T(8,128)(2,1)}, bf16[512,512]{1,0:T(8,128)(2,1)S(1)}, u32[]{:S(2)}, u32[]{:S(2)}) collective-permute-start(bf16[512,512]{1,0:T(8,128)(2,1)} %refs_4_.1), channel_id=1, source_target_pairs={{0,8},{4,12},{8,16},{12,20},{16,24},{20,28},{24,0},{28,4},{1,9},{5... | collective-permute-start | bytes 1572872 | tf_op jit(solution)/shard_map/ppermute | solution.py:243
  8.0 26.6 %collective-permute-start.16 = (bf16[512,512]{1,0:T(8,128)(2,1)}, bf16[512,512]{1,0:T(8,128)(2,1)S(1)}, u32[]{:S(2)}, u32[]{:S(2)}) collective-permute-start(bf16[512,512]{1,0:T(8,128)(2,1)} %refs_4_.1), channel_id=1, source_target_pairs={{0,24},{4,28},{8,0},{12,4},{16,8},{20,12},{24,16},{28,20},{1,25},{... | collective-permute-start | bytes 1572872 | tf_op jit(solution)/shard_map/ppermute | solution.py:243
  10.1 1.2 copy-start.1
  18.8 64.2 %copy-start.5 = (bf16[2,512,128]{2,1,0:T(8,128)(2,1)}, bf16[2,512,128]{2,1,0:T(8,128)(2,1)S(1)}, u32[]{:S(2)}) copy-start(bf16[2,512,128]{2,1,0:T(8,128)(2,1)S(1)} %pad_maximum_fusion.refs_0_) | copy-start | bytes 786436
  18.8 15.9 %collective-permute-start.2 = (bf16[2,512,128]{2,1,0:T(8,128)(2,1)S(1)}, bf16[2,512,128]{2,1,0:T(8,128)(2,1)S(1)}, u32[]{:S(2)}, u32[]{:S(2)}) collective-permute-start(bf16[2,512,128]{2,1,0:T(8,128)(2,1)S(1)} %pad_maximum_fusion.refs_0_), channel_id=1, source_target_pairs={{0,2},{1,3},{2,0},{3,1},{4,6},{5,7},{6,4},{7,5},{8,10},{9,11},{10,... | collective-permute-start | bytes 786440 | tf_op jit(solution)/shard_map/ppermute | solution.py:251
  20.9 15.4 %collective-permute-start.3 = (bf16[2,512,128]{2,1,0:T(8,128)(2,1)S(1)}, bf16[2,512,128]{2,1,0:T(8,128)(2,1)S(1)}, u32[]{:S(2)}, u32[]{:S(2)}) collective-permute-start(bf16[2,512,128]{2,1,0:T(8,128)(2,1)S(1)} %pad_maximum_fusion.refs_0_), channel_id=1, source_target_pairs={{0,1},{1,0},{2,3},{3,2},{4,5},{5,4},{6,7},{7,6},{8,9},{9,8},{10,11... | collective-permute-start | bytes 786440 | tf_op jit(solution)/shard_map/ppermute | solution.py:251
  29.1 53.9 %copy-start.9 = (bf16[512,512]{1,0:T(8,128)(2,1)}, bf16[512,512]{1,0:T(8,128)(2,1)S(1)}, u32[]{:S(2)}) copy-start(bf16[512,512]{1,0:T(8,128)(2,1)S(1)} %collective-permute-done.5.refs_5_) | copy-start | bytes 1572868
  29.1 11.0 %collective-permute-start.6 = (bf16[2,512,128]{2,1,0:T(8,128)(2,1)S(1)}, bf16[2,512,128]{2,1,0:T(8,128)(2,1)S(1)}, u32[]{:S(2)}, u32[]{:S(2)}) collective-permute-start(bf16[2,512,128]{2,1,0:T(8,128)(2,1)S(1)} %pad_maximum_fusion.1), channel_id=1, source_target_pairs={{0,8},{4,12},{8,16},{12,20},{16,24},{20,28},{24,0},{28,4},{1,9},{5... | collective-permute-start | bytes 786440 | tf_op jit(solution)/shard_map/ppermute | solution.py:243
  31.0 56.9 %copy-start.8 = (bf16[512,512]{1,0:T(8,128)(2,1)}, bf16[512,512]{1,0:T(8,128)(2,1)S(1)}, u32[]{:S(2)}) copy-start(bf16[512,512]{1,0:T(8,128)(2,1)S(1)} %collective-permute-done.10.refs_4_) | copy-start | bytes 1572868
  31.0 19.0 %collective-permute-start.12 = (bf16[2,512,128]{2,1,0:T(8,128)(2,1)S(1)}, bf16[2,512,128]{2,1,0:T(8,128)(2,1)S(1)}, u32[]{:S(2)}, u32[]{:S(2)}) collective-permute-start(bf16[2,512,128]{2,1,0:T(8,128)(2,1)S(1)} %pad_maximum_fusion.2), channel_id=1, source_target_pairs={{0,24},{4,28},{8,0},{12,4},{16,8},{20,12},{24,16},{28,20},{1,25},{... | collective-permute-start | bytes 786440 | tf_op jit(solution)/shard_map/ppermute | solution.py:243
  34.7 58.2 %copy-start.7 = (bf16[512,512]{1,0:T(8,128)(2,1)}, bf16[512,512]{1,0:T(8,128)(2,1)S(1)}, u32[]{:S(2)}) copy-start(bf16[512,512]{1,0:T(8,128)(2,1)S(1)} %collective-permute-done.16.refs_4_) | copy-start | bytes 1572868
  34.7 32.0 %collective-permute-start.18 = (bf16[2,512,128]{2,1,0:T(8,128)(2,1)S(1)}, bf16[2,512,128]{2,1,0:T(8,128)(2,1)S(1)}, u32[]{:S(2)}, u32[]{:S(2)}) collective-permute-start(bf16[2,512,128]{2,1,0:T(8,128)(2,1)S(1)} %pad_maximum_fusion.3), channel_id=1, source_target_pairs={{0,16},{4,20},{8,24},{12,28},{16,0},{20,4},{24,8},{28,12},{1,17},{... | collective-permute-start | bytes 786440 | tf_op jit(solution)/shard_map/ppermute | solution.py:243
  34.7 48.3 %copy-start.14 = (bf16[2,512,128]{2,1,0:T(8,128)(2,1)}, bf16[2,512,128]{2,1,0:T(8,128)(2,1)S(1)}, u32[]{:S(2)}) copy-start(bf16[2,512,128]{2,1,0:T(8,128)(2,1)S(1)} %collective-permute-done.2.refs_1_) | copy-start | bytes 786436
  34.7 35.2 %collective-permute-start.11 = (bf16[512,512]{1,0:T(8,128)(2,1)S(1)}, bf16[512,512]{1,0:T(8,128)(2,1)S(1)}, u32[]{:S(2)}, u32[]{:S(2)}) collective-permute-start(bf16[512,512]{1,0:T(8,128)(2,1)S(1)} %collective-permute-done.10.refs_4_), channel_id=1, source_target_pairs={{0,4},{4,0},{8,12},{12,8},{16,20},{20,16},{24,28},{28,24},{1,5},{5... | collective-permute-start | bytes 1572872 | tf_op jit(solution)/shard_map/ppermute | solution.py:247
  36.3 0.7 copy-start.15
  36.3 30.4 %collective-permute-start.4 = (bf16[2,512,128]{2,1,0:T(8,128)(2,1)S(1)}, bf16[2,512,128]{2,1,0:T(8,128)(2,1)S(1)}, u32[]{:S(2)}, u32[]{:S(2)}) collective-permute-start(bf16[2,512,128]{2,1,0:T(8,128)(2,1)S(1)} %collective-permute-done.2.refs_1_), channel_id=1, source_target_pairs={{0,1},{1,0},{2,3},{3,2},{4,5},{5,4},{6,7},{7,6},{8,9},{9,8},{10,11... | collective-permute-start | bytes 786440 | tf_op jit(solution)/shard_map/ppermute | solution.py:251
  40.1 41.0 %copy-start.16 = (bf16[2,512,128]{2,1,0:T(8,128)(2,1)}, bf16[2,512,128]{2,1,0:T(8,128)(2,1)S(1)}, u32[]{:S(2)}) copy-start(bf16[2,512,128]{2,1,0:T(8,128)(2,1)S(1)} %collective-permute-done.6.refs_0_) | copy-start | bytes 786436
  40.1 35.9 %collective-permute-start.22 = (bf16[512,512]{1,0:T(8,128)(2,1)S(1)}, bf16[512,512]{1,0:T(8,128)(2,1)S(1)}, u32[]{:S(2)}, u32[]{:S(2)}) collective-permute-start(bf16[512,512]{1,0:T(8,128)(2,1)S(1)} %collective-permute-done.10.refs_4_), channel_id=1, source_target_pairs={{0,8},{4,12},{8,16},{12,20},{16,24},{20,28},{24,0},{28,4},{1,9},{5... | collective-permute-start | bytes 1572872 | tf_op jit(solution)/shard_map/ppermute | solution.py:243
  50.0 31.1 %copy-start.17 = (bf16[2,512,128]{2,1,0:T(8,128)(2,1)}, bf16[2,512,128]{2,1,0:T(8,128)(2,1)S(1)}, u32[]{:S(2)}) copy-start(bf16[2,512,128]{2,1,0:T(8,128)(2,1)S(1)} %collective-permute-done.12.refs_0_) | copy-start | bytes 786436
  50.0 18.2 %collective-permute-start.7 = (bf16[2,512,128]{2,1,0:T(8,128)(2,1)S(1)}, bf16[2,512,128]{2,1,0:T(8,128)(2,1)S(1)}, u32[]{:S(2)}, u32[]{:S(2)}) collective-permute-start(bf16[2,512,128]{2,1,0:T(8,128)(2,1)S(1)} %collective-permute-done.6.refs_0_), channel_id=1, source_target_pairs={{0,2},{1,3},{2,0},{3,1},{4,6},{5,7},{6,4},{7,5},{8,10},{9,11},{10,... | collective-permute-start | bytes 786440 | tf_op jit(solution)/shard_map/ppermute | solution.py:251
  66.7 32.1 %copy-start.13 = (bf16[2,512,128]{2,1,0:T(8,128)(2,1)}, bf16[2,512,128]{2,1,0:T(8,128)(2,1)S(1)}, u32[]{:S(2)}) copy-start(bf16[2,512,128]{2,1,0:T(8,128)(2,1)S(1)} %collective-permute-done.18.refs_0_) | copy-start | bytes 786436
  66.7 1.7 collective-permute-start.8
  66.7 14.5 %copy-start.18 = (bf16[2,512,128]{2,1,0:T(8,128)(2,1)}, bf16[2,512,128]{2,1,0:T(8,128)(2,1)S(1)}, u32[]{:S(2)}) copy-start(bf16[2,512,128]{2,1,0:T(8,128)(2,1)S(1)} %collective-permute-done.4.refs_3_) | copy-start | bytes 786436
  66.7 9.3 %collective-permute-start.13 = (bf16[2,512,128]{2,1,0:T(8,128)(2,1)S(1)}, bf16[2,512,128]{2,1,0:T(8,128)(2,1)}, u32[]{:S(2)}, u32[]{:S(2)}) collective-permute-start(bf16[2,512,128]{2,1,0:T(8,128)(2,1)S(1)} %collective-permute-done.12.refs_0_), channel_id=1, source_target_pairs={{0,2},{1,3},{2,0},{3,1},{4,6},{5,7},{6,4},{7,5},{8,10},{9,11},{10,... | collective-permute-start | bytes 786440 | tf_op jit(solution)/shard_map/ppermute | solution.py:251
  68.2 12.9 %copy-start.19 = (bf16[2,512,128]{2,1,0:T(8,128)(2,1)}, bf16[2,512,128]{2,1,0:T(8,128)(2,1)S(1)}, u32[]{:S(2)}) copy-start(bf16[2,512,128]{2,1,0:T(8,128)(2,1)S(1)} %collective-permute-done.7.refs_1_) | copy-start | bytes 786436
  68.2 9.4 %collective-permute-start.14 = (bf16[2,512,128]{2,1,0:T(8,128)(2,1)S(1)}, bf16[2,512,128]{2,1,0:T(8,128)(2,1)S(1)}, u32[]{:S(2)}, u32[]{:S(2)}) collective-permute-start(bf16[2,512,128]{2,1,0:T(8,128)(2,1)S(1)} %collective-permute-done.12.refs_0_), channel_id=1, source_target_pairs={{0,1},{1,0},{2,3},{3,2},{4,5},{5,4},{6,7},{7,6},{8,9},{9,8},{10,11... | collective-permute-start | bytes 786440 | tf_op jit(solution)/shard_map/ppermute | solution.py:251
  68.4 12.8 %copy-start.20 = (bf16[2,512,128]{2,1,0:T(8,128)(2,1)}, bf16[2,512,128]{2,1,0:T(8,128)(2,1)S(1)}, u32[]{:S(2)}) copy-start(bf16[2,512,128]{2,1,0:T(8,128)(2,1)S(1)} %collective-permute-done.8.refs_2_) | copy-start | bytes 786436
  68.4 24.5 %collective-permute-start.17 = (bf16[512,512]{1,0:T(8,128)(2,1)S(1)}, bf16[512,512]{1,0:T(8,128)(2,1)}, u32[]{:S(2)}, u32[]{:S(2)}) collective-permute-start(bf16[512,512]{1,0:T(8,128)(2,1)S(1)} %collective-permute-done.16.refs_4_), channel_id=1, source_target_pairs={{0,4},{4,0},{8,12},{12,8},{16,20},{20,16},{24,28},{28,24},{1,5},{5... | collective-permute-start | bytes 1572872 | tf_op jit(solution)/shard_map/ppermute | solution.py:247
  69.9 18.0 %copy-start.11 = (bf16[512,512]{1,0:T(8,128)(2,1)}, bf16[512,512]{1,0:T(8,128)(2,1)S(1)}, u32[]{:S(2)}) copy-start(bf16[512,512]{1,0:T(8,128)(2,1)S(1)} %collective-permute-done.11.refs_5_) | copy-start | bytes 1572868
  69.9 11.2 %collective-permute-start.19 = (bf16[2,512,128]{2,1,0:T(8,128)(2,1)S(1)}, bf16[2,512,128]{2,1,0:T(8,128)(2,1)}, u32[]{:S(2)}, u32[]{:S(2)}) collective-permute-start(bf16[2,512,128]{2,1,0:T(8,128)(2,1)S(1)} %collective-permute-done.18.refs_0_), channel_id=1, source_target_pairs={{0,2},{1,3},{2,0},{3,1},{4,6},{5,7},{6,4},{7,5},{8,10},{9,11},{10,... | collective-permute-start | bytes 786440 | tf_op jit(solution)/shard_map/ppermute | solution.py:251
  76.0 5.1 %collective-permute-start.9 = (bf16[2,512,128]{2,1,0:T(8,128)(2,1)S(1)}, bf16[2,512,128]{2,1,0:T(8,128)(2,1)S(1)}, u32[]{:S(2)}, u32[]{:S(2)}) collective-permute-start(bf16[2,512,128]{2,1,0:T(8,128)(2,1)S(1)} %collective-permute-done.7.refs_1_), channel_id=1, source_target_pairs={{0,1},{1,0},{2,3},{3,2},{4,5},{5,4},{6,7},{7,6},{8,9},{9,8},{10,11... | collective-permute-start | bytes 786440 | tf_op jit(solution)/shard_map/ppermute | solution.py:251
  76.0 22.7 %copy-start.10 = (bf16[512,512]{1,0:T(8,128)(2,1)}, bf16[512,512]{1,0:T(8,128)(2,1)S(1)}, u32[]{:S(2)}) copy-start(bf16[512,512]{1,0:T(8,128)(2,1)S(1)} %collective-permute-done.22.refs_4_) | copy-start | bytes 1572868
  76.0 22.7 %collective-permute-start.23 = (bf16[512,512]{1,0:T(8,128)(2,1)S(1)}, bf16[512,512]{1,0:T(8,128)(2,1)}, u32[]{:S(2)}, u32[]{:S(2)}) collective-permute-start(bf16[512,512]{1,0:T(8,128)(2,1)S(1)} %collective-permute-done.22.refs_4_), channel_id=1, source_target_pairs={{0,4},{4,0},{8,12},{12,8},{16,20},{20,16},{24,28},{28,24},{1,5},{5... | collective-permute-start | bytes 1572872 | tf_op jit(solution)/shard_map/ppermute | solution.py:247
  77.6 3.5 %copy-start.21 = (bf16[2,512,128]{2,1,0:T(8,128)(2,1)}, bf16[2,512,128]{2,1,0:T(8,128)(2,1)S(1)}, u32[]{:S(2)}) copy-start(bf16[2,512,128]{2,1,0:T(8,128)(2,1)S(1)} %collective-permute-done.14.refs_2_) | copy-start | bytes 786436
  77.6 15.2 %collective-permute-start.15 = (bf16[2,512,128]{2,1,0:T(8,128)(2,1)}, bf16[2,512,128]{2,1,0:T(8,128)(2,1)}, u32[]{:S(2)}, u32[]{:S(2)}) collective-permute-start(bf16[2,512,128]{2,1,0:T(8,128)(2,1)} %collective-permute-done.13.refs_1_), channel_id=1, source_target_pairs={{0,1},{1,0},{2,3},{3,2},{4,5},{5,4},{6,7},{7,6},{8,9},{9,8},{10,11... | collective-permute-start | bytes 786440 | tf_op jit(solution)/shard_map/ppermute | solution.py:251
  81.1 17.6 %collective-permute-start.20 = (bf16[2,512,128]{2,1,0:T(8,128)(2,1)S(1)}, bf16[2,512,128]{2,1,0:T(8,128)(2,1)}, u32[]{:S(2)}, u32[]{:S(2)}) collective-permute-start(bf16[2,512,128]{2,1,0:T(8,128)(2,1)S(1)} %collective-permute-done.18.refs_0_), channel_id=1, source_target_pairs={{0,1},{1,0},{2,3},{3,2},{4,5},{5,4},{6,7},{7,6},{8,9},{9,8},{10,11... | collective-permute-start | bytes 786440 | tf_op jit(solution)/shard_map/ppermute | solution.py:251
  81.2 0.7 copy-start.22
  81.9 16.8 %collective-permute-start.21 = (bf16[2,512,128]{2,1,0:T(8,128)(2,1)}, bf16[2,512,128]{2,1,0:T(8,128)(2,1)}, u32[]{:S(2)}, u32[]{:S(2)}) collective-permute-start(bf16[2,512,128]{2,1,0:T(8,128)(2,1)} %collective-permute-done.19.refs_1_), channel_id=1, source_target_pairs={{0,1},{1,0},{2,3},{3,2},{4,5},{5,4},{6,7},{7,6},{8,9},{9,8},{10,11... | collective-permute-start | bytes 786440 | tf_op jit(solution)/shard_map/ppermute | solution.py:251
  92.8 12.9 %copy-start.23 = (f32[8,128]{1,0:T(8,128)S(1)}, f32[8,128]{1,0:T(8,128)}, u32[]{:S(2)}) copy-start(f32[8,128]{1,0:T(8,128)} %get-tuple-element.15) | copy-start | bytes 12292
  92.8 12.9 %copy-start.24 = (f32[8,128]{1,0:T(8,128)S(1)}, f32[8,128]{1,0:T(8,128)}, u32[]{:S(2)}) copy-start(f32[8,128]{1,0:T(8,128)} %get-tuple-element.17) | copy-start | bytes 12292
  92.8 17.1 %copy-start.2 = (bf16[512,512]{1,0:T(8,128)(2,1)S(1)}, bf16[512,512]{1,0:T(8,128)(2,1)}, u32[]{:S(2)}) copy-start(bf16[512,512]{1,0:T(8,128)(2,1)} %refs_4_.1) | copy-start | bytes 1572868
  98.7 7.1 %copy-start.25 = (f32[8,128]{1,0:T(8,128)S(1)}, f32[8,128]{1,0:T(8,128)}, u32[]{:S(2)}) copy-start(f32[8,128]{1,0:T(8,128)} %get-tuple-element.19) | copy-start | bytes 12292
  107.2 11.1 %all-to-all-start = ((f32[32,8,128]{2,1,0:T(8,128)}), f32[32,8,128]{2,1,0:T(8,128)S(1)}, u32[]{:S(2)}, u32[]{:S(2)}) async-start(f32[32,8,128]{2,1,0:T(8,128)} %broadcast_in_dim.2), calls=%async_computation | async-start | bytes 262144 | tf_op jit(solution)/shard_map/all_to_all | solution.py:332
  110.0 21.7 %collective-permute-start = (bf16[512,512]{1,0:T(8,128)(2,1)S(1)}, bf16[512,512]{1,0:T(8,128)(2,1)S(1)}, u32[]{:S(2)}, u32[]{:S(2)}) collective-permute-start(bf16[512,512]{1,0:T(8,128)(2,1)S(1)} %copy-done.2), channel_id=1, source_target_pairs={{0,1},{1,0},{2,3},{3,2},{4,5},{5,4},{6,7},{7,6},{8,9},{9,8},{10,11... | collective-permute-start | bytes 1572872 | tf_op jit(solution)/shard_map/ppermute | solution.py:251
  110.3 23.0 %collective-permute-start.26 = (bf16[512,512]{1,0:T(8,128)(2,1)S(1)}, bf16[512,512]{1,0:T(8,128)(2,1)S(1)}, u32[]{:S(2)}, u32[]{:S(2)}) collective-permute-start(bf16[512,512]{1,0:T(8,128)(2,1)S(1)} %copy-done.2), channel_id=1, source_target_pairs={{0,2},{1,3},{2,0},{3,1},{4,6},{5,7},{6,4},{7,5},{8,10},{9,11},{10,... | collective-permute-start | bytes 1572872 | tf_op jit(solution)/shard_map/ppermute | solution.py:251
  118.2 0.7 copy-start.6
  127.2 16.0 %collective-permute-start.24 = (f16[512,512]{1,0:T(8,128)(2,1)}, f16[512,512]{1,0:T(8,128)(2,1)S(1)}, u32[]{:S(2)}, u32[]{:S(2)}) collective-permute-start(f16[512,512]{1,0:T(8,128)(2,1)} %convert_element_type.102), channel_id=1, source_target_pairs={{0,8},{4,12},{8,16},{12,20},{16,24},{20,28},{24,0},{28,4},{1,9},{5... | collective-permute-start | bytes 1572872 | tf_op jit(solution)/shard_map/ppermute | solution.py:243
  131.5 26.1 %collective-permute-start.25 = (bf16[1024,512]{1,0:T(8,128)(2,1)}, bf16[1024,512]{1,0:T(8,128)(2,1)}, u32[]{:S(2)}, u32[]{:S(2)}) collective-permute-start(bf16[1024,512]{1,0:T(8,128)(2,1)} %get-tuple-element.30), channel_id=1, source_target_pairs={{0,1},{1,0},{2,3},{3,2},{4,5},{5,4},{6,7},{7,6},{8,9},{9,8},{10,11... | collective-permute-start | bytes 3145736 | tf_op jit(solution)/shard_map/ppermute | solution.py:251
  131.5 28.1 %collective-permute-start.28 = (bf16[1024,512]{1,0:T(8,128)(2,1)}, bf16[1024,512]{1,0:T(8,128)(2,1)}, u32[]{:S(2)}, u32[]{:S(2)}) collective-permute-start(bf16[1024,512]{1,0:T(8,128)(2,1)} %get-tuple-element.32), channel_id=1, source_target_pairs={{0,2},{1,3},{2,0},{3,1},{4,6},{5,7},{6,4},{7,5},{8,10},{9,11},{10,... | collective-permute-start | bytes 3145736 | tf_op jit(solution)/shard_map/ppermute | solution.py:251
  131.6 11.5 %copy-start.3 = (bf16[512,512]{1,0:T(8,128)(2,1)}, bf16[512,512]{1,0:T(8,128)(2,1)S(1)}, u32[]{:S(2)}) copy-start(bf16[512,512]{1,0:T(8,128)(2,1)S(1)} %collective-permute-done) | copy-start | bytes 1572868
  131.6 47.7 %collective-permute-start.30 = (bf16[1024,512]{1,0:T(8,128)(2,1)}, bf16[1024,512]{1,0:T(8,128)(2,1)}, u32[]{:S(2)}, u32[]{:S(2)}) collective-permute-start(bf16[1024,512]{1,0:T(8,128)(2,1)} %get-tuple-element.31), channel_id=1, source_target_pairs={{0,3},{1,2},{2,1},{3,0},{4,7},{5,6},{6,5},{7,4},{8,11},{9,10},{10,... | collective-permute-start | bytes 3145736 | tf_op jit(solution)/shard_map/ppermute | solution.py:251
  133.3 24.2 %collective-permute-start.29 = (bf16[512,512]{1,0:T(8,128)(2,1)S(1)}, bf16[512,512]{1,0:T(8,128)(2,1)}, u32[]{:S(2)}, u32[]{:S(2)}) collective-permute-start(bf16[512,512]{1,0:T(8,128)(2,1)S(1)} %collective-permute-done.26), channel_id=1, source_target_pairs={{0,1},{1,0},{2,3},{3,2},{4,5},{5,4},{6,7},{7,6},{8,9},{9,8},{10,11... | collective-permute-start | bytes 1572872 | tf_op jit(solution)/shard_map/ppermute | solution.py:251
  143.2 0.8 copy-start.12
  144.0 13.4 %collective-permute-start.27 = (f16[512,512]{1,0:T(8,128)(2,1)}, f16[512,512]{1,0:T(8,128)(2,1)}, u32[]{:S(2)}, u32[]{:S(2)}) collective-permute-start(f16[512,512]{1,0:T(8,128)(2,1)} %convert_element_type.102), channel_id=1, source_target_pairs={{0,24},{4,28},{8,0},{12,4},{16,8},{20,12},{24,16},{28,20},{1,25},{... | collective-permute-start | bytes 1572872 | tf_op jit(solution)/shard_map/ppermute | solution.py:243
  145.9 11.6 %copy-start.4 = (bf16[512,512]{1,0:T(8,128)(2,1)S(1)}, bf16[512,512]{1,0:T(8,128)(2,1)}, u32[]{:S(2)}) copy-start(bf16[512,512]{1,0:T(8,128)(2,1)} %copy-done.3) | copy-start | bytes 1572868
  157.4 33.8 %collective-permute-start.32 = (f16[512,512]{1,0:T(8,128)(2,1)}, f16[512,512]{1,0:T(8,128)(2,1)}, u32[]{:S(2)}, u32[]{:S(2)}) collective-permute-start(f16[512,512]{1,0:T(8,128)(2,1)} %convert_element_type.102), channel_id=1, source_target_pairs={{0,4},{4,0},{8,12},{12,8},{16,20},{20,16},{24,28},{28,24},{1,5},{5... | collective-permute-start | bytes 1572872 | tf_op jit(solution)/shard_map/ppermute | solution.py:247
  184.7 16.2 %collective-permute-start.31 = (f16[512,512]{1,0:T(8,128)(2,1)}, f16[512,512]{1,0:T(8,128)(2,1)S(1)}, u32[]{:S(2)}, u32[]{:S(2)}) collective-permute-start(f16[512,512]{1,0:T(8,128)(2,1)} %copy-done.12), channel_id=1, source_target_pairs={{0,8},{4,12},{8,16},{12,20},{16,24},{20,28},{24,0},{28,4},{1,9},{5... | collective-permute-start | bytes 1572872 | tf_op jit(solution)/shard_map/ppermute | solution.py:243
  185.3 18.9 %collective-permute-start.33 = (f16[512,512]{1,0:T(8,128)(2,1)}, f16[512,512]{1,0:T(8,128)(2,1)S(1)}, u32[]{:S(2)}, u32[]{:S(2)}) collective-permute-start(f16[512,512]{1,0:T(8,128)(2,1)} %copy-done.12), channel_id=1, source_target_pairs={{0,4},{4,0},{8,12},{12,8},{16,20},{20,16},{24,28},{28,24},{1,5},{5... | collective-permute-start | bytes 1572872 | tf_op jit(solution)/shard_map/ppermute | solution.py:247
  185.9 25.6 %collective-permute-start.34 = (f16[512,512]{1,0:T(8,128)(2,1)}, f16[512,512]{1,0:T(8,128)(2,1)S(1)}, u32[]{:S(2)}, u32[]{:S(2)}) collective-permute-start(f16[512,512]{1,0:T(8,128)(2,1)} %collective-permute-done.27), channel_id=1, source_target_pairs={{0,4},{4,0},{8,12},{12,8},{16,20},{20,16},{24,28},{28,24},{1,5},{5... | collective-permute-start | bytes 1572872 | tf_op jit(solution)/shard_map/ppermute | solution.py:247
  200.9 21.0 %collective-permute-start.35 = (f16[512,512]{1,0:T(8,128)(2,1)S(1)}, f16[512,512]{1,0:T(8,128)(2,1)S(1)}, u32[]{:S(2)}, u32[]{:S(2)}) collective-permute-start(f16[512,512]{1,0:T(8,128)(2,1)S(1)} %collective-permute-done.31), channel_id=1, source_target_pairs={{0,4},{4,0},{8,12},{12,8},{16,20},{20,16},{24,28},{28,24},{1,5},{5... | collective-permute-start | bytes 1572872 | tf_op jit(solution)/shard_map/ppermute | solution.py:247
where the time goes:
time: 224 us
  waiting for transfers between devices  105 us (47%)
  starting transfers between devices  45.4 us (20%)
  Pallas kernels  30.4 us (14%)
  local copies, waits for them, and re-layouts  20 us (9%)
  other arithmetic  13.2 us (6%)
  matrix products  8.09 us (4%)
    ppermute x9, waiting for transfers between devices, along_z(): return lax.ppermute(value, 'dp', ring)  44.1 us
    ppermute x9, waiting for transfers between devices, along_y(): return lax.ppermute(value, 'dp', ring)  28.7 us
    ppermute x18, waiting for transfers between devices, along_tensor(): return lax.ppermute(value, 'tensor', ring)  26 us
    pallas_call x4, Pallas kernels, exchanges(): pl.pallas_call(functools.partial(grads_kernel, inner, groups, at * inner)...  22.6 us
    ppermute x9, starting transfers between devices, along_z(): return lax.ppermute(value, 'dp', ring)  20.7 us
    ppermute x18, starting transfers between devices, along_tensor(): return lax.ppermute(value, 'tensor', ring)  11.3 us
    ppermute x9, starting transfers between devices, along_y(): return lax.ppermute(value, 'dp', ring)  10.6 us
    mul x8, other arithmetic, exchanges(): lines[k][l].reshape(groups, 1, width, columns).astype(jnp.float32)  10.2 us
  transfers between devices with their start and end apart: 37, of which 13 were waited for; matrix products, arithmetic and copies ran while one was open for 15% of the time, Pallas kernels for 10%

commit v1 on v0

--- a/solution.py
+++ b/solution.py
@@ -101,21 +101,24 @@
 def grads_kernel(replicas, groups, before, index_ref, *refs):
     slices, refs = refs[:groups], refs[groups:]
     cots, refs = refs[:replicas], refs[replicas:]
-    earlier, refs = refs[: before // replicas], refs[before // replicas :]
+    lines = before // replicas
+    earlier, refs = refs[:lines], refs[lines:]
+    total_ref, refs = (refs[0], refs[1:]) if lines else (None, refs)
     grads_ref, gram_ref, acts, cotangents, held, sems = refs
     width, columns = acts.shape[3], cotangents.shape[2]
-    lines = len(earlier)
+    count = index_ref.shape[0] - groups
     features = groups * width
     loads = fetch(
-        [(slices[m], acts.at[m]) for m in range(groups)]
-        + [(cots[l], cotangents.at[l]) for l in range(replicas)]
+        [(cots[l], cotangents.at[l]) for l in range(replicas)]
+        + [(slices[m], acts.at[m]) for m in range(groups)]
         + [(earlier[i], held.at[i]) for i in range(lines)],
         sems,
     )
-    for copy in loads[: groups + replicas]:
+    for copy in loads[:replicas]:
         copy.wait()
-    for l in range(replicas):
-        for m in range(groups):
+    for m in range(groups):
+        loads[replicas + m].wait()
+        for l in range(replicas):
             at = pl.multiple_of(index_ref[m] * width, width)
             held[lines, l, pl.ds(at, width), :] = lax.dot_general(
                 acts[m, l],
@@ -143,29 +146,38 @@
 
     zero = jnp.zeros((8, lanes), jnp.float32)
     sums = lax.fori_loop(0, features // 8, body, tuple(zero for _ in pairs))
-    row = lax.broadcasted_iota(jnp.int32, (8, lanes), 0)
-    col = lax.broadcasted_iota(jnp.int32, (8, lanes), 1)
-    gram = zero
+    col = lax.broadcasted_iota(jnp.int32, (1, lanes), 1)
+    gram = total_ref[0] if lines else jnp.zeros((1, lanes), jnp.float32)
     for (a, b), total in zip(pairs, sums):
         value = jnp.sum(jnp.sum(total, axis=0, keepdims=True), axis=1, keepdims=True)
         low = jnp.minimum(index_ref[groups + a], index_ref[groups + b])
         high = jnp.maximum(index_ref[groups + a], index_ref[groups + b])
-        gram = gram + jnp.where((row == low) & (col == high), value, 0.0)
-    gram_ref[...] = gram
+        gram = gram + jnp.where(col == low * count + high, value, 0.0)
+    gram_ref[...] = jnp.broadcast_to(gram[None], gram_ref.shape)
     store.wait()
 
 
 def combine_kernel(replicas, groups, index_ref, gram_ref, *refs):
     blocks, (piece_ref, scale_ref, held, sems) = refs[:-4], refs[-4:]
     count = len(blocks) * replicas
-    loads = fetch([(block, held.at[i]) for i, block in enumerate(blocks)], sems)
-    gram = jnp.sum(gram_ref[...], axis=0)
-    row = lax.broadcasted_iota(jnp.int32, gram.shape, 0)
+    features, _ = piece_ref.shape
+    chunks = 4
+    span = features // chunks
+    loads = fetch(
+        [
+            (block.at[:, pl.ds(c * span, span), :], held.at[i, :, pl.ds(c * span, span), :])
+            for c in range(chunks)
+            for i, block in enumerate(blocks)
+        ],
+        sems,
+    )
+    gram = gram_ref[0]
+    for source in range(1, gram_ref.shape[0]):
+        gram = gram + gram_ref[source]
     col = lax.broadcasted_iota(jnp.int32, gram.shape, 1)
 
     def entry(i, j):
-        found = jnp.where((row == i) & (col == j), gram, 0.0)
-        return jnp.sum(jnp.sum(found, axis=0, keepdims=True), axis=1, keepdims=True)
+        return jnp.sum(jnp.where(col == i * count + j, gram, 0.0), axis=1, keepdims=True)
 
     products = [[entry(i, j) if j >= i else None for j in range(count)] for i in range(count)]
     coefs = merge_coefs(products)
@@ -176,9 +188,6 @@
     for at in range(count):
         weight = sum(jnp.where(index_ref[groups + at] == i, coefs[i], 0.0) for i in range(count))
         weights.append(weight * (peak / bound))
-    features, _ = piece_ref.shape
-    for copy in loads:
-        copy.wait()
 
     def body(chunk, carry):
         at = pl.multiple_of(chunk * 16, 16)
@@ -190,7 +199,10 @@
         piece_ref[pl.ds(at, 16), :] = total
         return carry
 
-    lax.fori_loop(0, features // 16, body, 0)
+    for c in range(chunks):
+        for copy in loads[c * len(blocks) : (c + 1) * len(blocks)]:
+            copy.wait()
+        lax.fori_loop(c * span // 16, (c + 1) * span // 16, body, 0)
 
 
 def pack_kernel(index_ref, attention_ref, packed_ref):
@@ -238,35 +250,44 @@
     z, y = me // inner, me % inner
     x, core = part // 2, part % 2
 
-    def along_z(value, k):
-        ring = [(i * inner + j, (i + k) % outer * inner + j) for i in range(outer) for j in range(inner)]
+    def along_z(value, place):
+        ring = [(i * inner + j, place(i) * inner + j) for i in range(outer) for j in range(inner)]
         return lax.ppermute(value, "dp", ring)
 
     def along_y(value, l):
-        ring = [(i * inner + j, i * inner + (j + l) % inner) for i in range(outer) for j in range(inner)]
+        ring = [(i * inner + j, i * inner + (j ^ l)) for i in range(outer) for j in range(inner)]
         return lax.ppermute(value, "dp", ring)
 
     def along_tensor(value, j, flip):
         ring = [(a * 2 + c, (a + j) % pairs * 2 + (c ^ flip)) for a in range(pairs) for c in range(2)]
         return lax.ppermute(value, "tensor", ring)
 
-    right = outer // 2
-    arrival = [0, 1]
-    for k in range(1, right + 1):
-        arrival += [outer - k] if outer - k > right else []
-        arrival += [k + 1] if k < right else []
-
-    def gather_lines(value):
+    def along_both(found):
+        return {k: [found[k]] + [along_y(found[k], l) for l in range(1, inner)] for k in found}
+
+    def by_exchange(value):
         found = {0: value}
-        for k in arrival[1:]:
-            source, step = (found[(k + 1) % outer], -1) if k > right else (found[k - 1], 1)
-            found[k] = along_z(source, step)
-        return {k: [found[k]] + [along_y(found[k], l) for l in range(1, inner)] for k in arrival}
+        step = outer // 2
+        while step:
+            for k in list(found):
+                found[k ^ step] = along_z(found[k], lambda i: i ^ step)
+            step //= 2
+        return along_both({k: found[k] for k in range(outer)})
+
+    def by_ring(value):
+        found = {0: value, 1: along_z(value, lambda i: (i + 1) % outer)}
+        for k in range(2, outer // 2 + 1):
+            found[k] = along_z(found[k - 1], lambda i: (i + 1) % outer)
+        for k in range(outer - 1, outer // 2, -1):
+            found[k] = along_z(found[(k + 1) % outer], lambda i: (i - 1) % outer)
+        return along_both({k: found[k] for k in ring_order})
+
+    ring_order = [0, 1] + [k for k in range(outer - 1, outer // 2, -1)] + list(range(2, outer // 2 + 1))
 
     def replica_of(k, l):
-        return (z - k) % outer * inner + (y - l) % inner
-
-    cots = gather_lines(cotangent)
+        return (z ^ k) * inner + (y ^ l)
+
+    cots = by_exchange(cotangent)
 
     own_rows = projection.reshape(groups, -1, columns)
 
@@ -283,7 +304,7 @@
     cot_blocks.update({(j, 1): along_tensor(cot_blocks[j, 0], 0, 1) for j in range(pairs)})
 
     targets = [
-        jnp.stack([(z + k) % outer * inner + (y + l) % inner for k in range(outer)]).astype(jnp.int32)
+        jnp.stack([replica_of(k, l) for k in range(outer)]).astype(jnp.int32)
         for l in range(inner)
     ]
     from_y = [
@@ -291,28 +312,31 @@
         for l in range(inner)
     ]
     slices, slots = {}, []
-    for k in arrival:
+    for k in range(outer):
         held = jnp.stack([from_y[l][k] for l in range(inner)])
         if k:
-            held = along_z(held, k)
+            held = along_z(held, lambda i: i ^ k)
         shifted = [held] + [along_tensor(held, j, 0) for j in range(1, pairs)]
         slices[k] = shifted + [along_tensor(value, 0, 1) for value in shifted]
     for flip in (0, 1):
         slots += [(x - j) % pairs * 2 + (core ^ flip) for j in range(pairs)]
 
-    order = [replica_of(k, l) for k in arrival for l in range(inner)]
+    order = [replica_of(k, l) for k in range(outer) for l in range(inner)]
     index = jnp.stack([jnp.asarray(v, jnp.int32) for v in slots + order])
     grads, gram = [], None
     smem, hbm = pl.BlockSpec(memory_space=pltpu.SMEM), pl.BlockSpec(memory_space=pltpu.HBM)
-    for at, k in enumerate(arrival):
+    for at, k in enumerate(range(outer)):
         operands = [*slices[k], *cots[k], *grads]
-        block, partial = pl.pallas_call(
+        vmem = pl.BlockSpec(memory_space=pltpu.VMEM)
+        so_far = [gram] if grads else []
+        copies = n * groups if k == outer - 1 else 1
+        block, gram = pl.pallas_call(
             functools.partial(grads_kernel, inner, groups, at * inner),
-            in_specs=[smem] + [hbm] * len(operands),
-            out_specs=(hbm, pl.BlockSpec(memory_space=pltpu.VMEM)),
+            in_specs=[smem] + [hbm] * len(operands) + [vmem] * len(so_far),
+            out_specs=(hbm, vmem),
             out_shape=(
                 jax.ShapeDtypeStruct((inner, features, columns), jnp.float32),
-                jax.ShapeDtypeStruct((8, lanes), jnp.float32),
+                jax.ShapeDtypeStruct((copies, 1, lanes), jnp.float32),
             ),
             scratch_shapes=[
                 pltpu.VMEM((groups, inner, rows, width), attention.dtype),
@@ -325,13 +349,10 @@
                 bytes_accessed=8 * inner * features * columns,
                 transcendentals=0,
             ),
-        )(index, *operands)
+        )(index, *operands, *so_far)
         grads.append(block)
-        gram = partial if gram is None else gram + partial
-
-    shared = lax.all_to_all(
-        jnp.broadcast_to(gram[None], (n * groups, 8, lanes)), ("dp", "tensor"), 0, 0, tiled=True
-    ).reshape(n * groups, 8, lanes)
+
+    shared = lax.all_to_all(gram, ("dp", "tensor"), 0, 0, tiled=True).reshape(n * groups, 1, lanes)
     sent, scale = pl.pallas_call(
         functools.partial(combine_kernel, inner, groups),
         in_specs=[smem, pl.BlockSpec(memory_space=pltpu.VMEM)] + [hbm] * outer,
@@ -342,7 +363,7 @@
         ),
         scratch_shapes=[
             pltpu.VMEM((outer, inner, features, columns), jnp.float32),
-            pltpu.SemaphoreType.DMA((outer,)),
+            pltpu.SemaphoreType.DMA((4 * outer,)),
         ],
         cost_estimate=pl.CostEstimate(
             flops=2 * n * features * columns, bytes_accessed=4 * n * features * columns, transcendentals=0
@@ -350,18 +371,19 @@
         name="combine",
     )(index, shared, *grads)
     combined = unwritten((groups, n, width, columns))
-    lines = gather_lines(after(sent.astype(jnp.float16)))
+    lines = by_ring(after(sent.astype(jnp.float16)))
     for l in range(inner):
-        for k in arrival:
+        for k in ring_order:
             values = lines[k][l].reshape(groups, 1, width, columns).astype(jnp.float32) * scale[0, 0]
-            combined = lax.dynamic_update_slice_in_dim(combined, values, replica_of(k, l), 1)
+            source = (z - k) % outer * inner + (y ^ l)
+            combined = lax.dynamic_update_slice_in_dim(combined, values, source, 1)
     combined = combined.reshape(groups * n * width, columns)
 
     total = None
     for key in [(0, 0), (0, 1)] + [(j, flip) for j in range(1, pairs) for flip in (0, 1)]:
         theirs = cot_blocks[key]
         if key != (0, 0):
-            theirs = after(theirs, lines[outer - 1 if key[0] else 1][0])
+            theirs = after(theirs, lines[ring_order[2] if key[0] else 1][0])
         term = lax.dot_general(theirs, row_blocks[key], (((1,), (1,)), ((), ())), preferred_element_type=jnp.float32)
         total = term if total is None else total + term
     return (total.astype(jnp.bfloat16), combined)

time: 224 us -> 213 us (0.951)
  starting transfers between devices: 45.4 us -> 38.7 us
    ppermute x9, starting transfers between devices: 20.7 us -> 12.5 us  [along_z(): return lax.ppermute(value, 'dp', ring)]
    ppermute x9, waiting for transfers between devices: 44.1 us -> 39.7 us  [along_z(): return lax.ppermute(value, 'dp', ring)]
    ppermute x18, waiting for transfers between devices: 26 us -> 29.7 us  [along_tensor(): return lax.ppermute(value, 'tensor', ring)]
    unnamed x53 -> x45, local copies, waits for them, and re-layouts: 6.72 us -> 6.56 us
  transfers between devices with their start and end apart: 37 -> 37, of which waited for: 13 -> 13; matrix products, arithmetic and copies ran while one was open for 15% -> 15% of each run, Pallas kernels for 10% -> 11%
where the time goes in v1:
time: 213 us; the launch traced here: 212 us
  waiting for transfers between devices  103 us (48%)
  starting transfers between devices  38.7 us (18%)
  Pallas kernels  29.8 us (14%)
  local copies, waits for them, and re-layouts  19.2 us (9%)
  other arithmetic  12.5 us (6%)
  matrix products  8.09 us (4%)
    ppermute x9, waiting for transfers between devices, along_z(): return lax.ppermute(value, 'dp', ring)  39.7 us
    ppermute x18, waiting for transfers between devices, along_tensor(): return lax.ppermute(value, 'tensor', ring)  29.7 us
    ppermute x9, waiting for transfers between devices, along_y(): return lax.ppermute(value, 'dp', ring)  28.1 us
    pallas_call x4, Pallas kernels, exchanges(): pl.pallas_call(functools.partial(grads_kernel, inner, groups, at * inner)...  22.6 us
    ppermute x9, starting transfers between devices, along_z(): return lax.ppermute(value, 'dp', ring)  12.5 us
    ppermute x18, starting transfers between devices, along_tensor(): return lax.ppermute(value, 'tensor', ring)  11.4 us
    ppermute x9, starting transfers between devices, along_y(): return lax.ppermute(value, 'dp', ring)  10.8 us
    mul x8, other arithmetic, exchanges(): lines[k][l].reshape(groups, 1, width, columns).astype(jnp.float32)  10.2 us
  transfers between devices with their start and end apart: 37, of which 13 were waited for; matrix products, arithmetic and copies ran while one was open for 15% of the time, Pallas kernels for 11%

profile of v1, /device:TPU:0, one launch (start us, length us, event | category | flops | bytes accessed | tf_op | source)
XLA Modules:
  0.0 212.4 jit_solution(13104449693426472777)
XLA Ops:
  0.7 1.2 copy-done
  2.0 0.8 pack.3
  2.8 3.1 %collective-permute-start.1 = (bf16[4,512,128]{2,1,0:T(8,128)(2,1)S(1)}, bf16[4,512,128]{2,1,0:T(8,128)(2,1)S(1)}, u32[]{:S(2)}, u32[]{:S(2)}) collective-permute-start(bf16[4,512,128]{2,1,0:T(8,128)(2,1)S(1)} %pack.3), channel_id=1, source_target_pairs={{0,4},{4,0},{8,12},{12,8},{16,20},{20,16},{24,28},{28,24},{1,5},{5... | collective-permute-start | bytes 1572872 | tf_op jit(solution)/shard_map/ppermute | solution.py:259
  6.0 2.0 collective-permute-start.17
  8.0 2.6 %collective-permute-start.6 = (bf16[512,512]{1,0:T(8,128)(2,1)}, bf16[512,512]{1,0:T(8,128)(2,1)}, u32[]{:S(2)}, u32[]{:S(2)}) collective-permute-start(bf16[512,512]{1,0:T(8,128)(2,1)} %refs_4_.1), channel_id=1, source_target_pairs={{0,16},{4,20},{8,24},{12,28},{16,0},{20,4},{24,8},{28,12},{1,17},{... | collective-permute-start | bytes 1572872 | tf_op jit(solution)/shard_map/ppermute | solution.py:255
  10.6 1.2 copy-done.1
  11.8 0.8 pack.2
  12.7 6.0 %collective-permute-done.1 = bf16[4,512,128]{2,1,0:T(8,128)(2,1)S(1)} collective-permute-done((bf16[4,512,128]{2,1,0:T(8,128)(2,1)S(1)}, bf16[4,512,128]{2,1,0:T(8,128)(2,1)S(1)}, u32[]{:S(2)}, u32[]{:S(2)}) %collective-permute-start.1) | collective-permute-done | bytes 524320 | tf_op jit(solution)/shard_map/ppermute | solution.py:259
  18.7 2.1 collective-permute-start.9
  20.8 8.2 %collective-permute-done.12.refs_5_ = bf16[512,512]{1,0:T(8,128)(2,1)S(1)} collective-permute-done((bf16[512,512]{1,0:T(8,128)(2,1)}, bf16[512,512]{1,0:T(8,128)(2,1)S(1)}, u32[]{:S(2)}, u32[]{:S(2)}) %collective-permute-start.12) | collective-permute-done | bytes 524320 | tf_op jit(solution)/shard_map/ppermute | solution.py:259
  29.0 1.8 collective-permute-start.13
  30.9 2.7 %collective-permute-start.19 = (bf16[2,512,128]{2,1,0:T(8,128)(2,1)S(1)}, bf16[2,512,128]{2,1,0:T(8,128)(2,1)S(1)}, u32[]{:S(2)}, u32[]{:S(2)}) collective-permute-start(bf16[2,512,128]{2,1,0:T(8,128)(2,1)S(1)} %pad_maximum_fusion.3), channel_id=1, source_target_pairs={{0,16},{4,20},{8,24},{12,28},{16,0},{20,4},{24,8},{28,12},{1,17},{... | collective-permute-start | bytes 786440 | tf_op jit(solution)/shard_map/ppermute | solution.py:255
  33.6 2.3 %collective-permute-start.2 = (bf16[2,512,128]{2,1,0:T(8,128)(2,1)S(1)}, bf16[2,512,128]{2,1,0:T(8,128)(2,1)S(1)}, u32[]{:S(2)}, u32[]{:S(2)}) collective-permute-start(bf16[2,512,128]{2,1,0:T(8,128)(2,1)S(1)} %pad_maximum_fusion), channel_id=1, source_target_pairs={{0,24},{4,28},{8,16},{12,20},{16,8},{20,12},{24,0},{28,4},{1,25},{... | collective-permute-start | bytes 786440 | tf_op jit(solution)/shard_map/ppermute | solution.py:255
  35.9 1.5 collective-permute-start.18
  37.4 0.7 copy-done.13
  38.1 3.1 %collective-permute-done.13.refs_0_ = bf16[2,512,128]{2,1,0:T(8,128)(2,1)S(1)} collective-permute-done((bf16[2,512,128]{2,1,0:T(8,128)(2,1)S(1)}, bf16[2,512,128]{2,1,0:T(8,128)(2,1)S(1)}, u32[]{:S(2)}, u32[]{:S(2)}) %collective-permute-start.13) | collective-permute-done | bytes 262176 | tf_op jit(solution)/shard_map/ppermute | solution.py:255
  41.2 11.1 %collective-permute-done.19.refs_0_ = bf16[2,512,128]{2,1,0:T(8,128)(2,1)S(1)} collective-permute-done((bf16[2,512,128]{2,1,0:T(8,128)(2,1)S(1)}, bf16[2,512,128]{2,1,0:T(8,128)(2,1)S(1)}, u32[]{:S(2)}, u32[]{:S(2)}) %collective-permute-start.19) | collective-permute-done | bytes 262176 | tf_op jit(solution)/shard_map/ppermute | solution.py:255
  52.3 1.5 collective-permute-start.14
  54.5 6.0 %collective-permute-done.14.refs_1_ = bf16[2,512,128]{2,1,0:T(8,128)(2,1)S(1)} collective-permute-done((bf16[2,512,128]{2,1,0:T(8,128)(2,1)S(1)}, bf16[2,512,128]{2,1,0:T(8,128)(2,1)S(1)}, u32[]{:S(2)}, u32[]{:S(2)}) %collective-permute-start.14) | collective-permute-done | bytes 262176 | tf_op jit(solution)/shard_map/ppermute | solution.py:263
  60.5 1.6 collective-permute-start.23
  62.1 2.5 %collective-permute-start.3 = (bf16[2,512,128]{2,1,0:T(8,128)(2,1)S(1)}, bf16[2,512,128]{2,1,0:T(8,128)(2,1)}, u32[]{:S(2)}, u32[]{:S(2)}) collective-permute-start(bf16[2,512,128]{2,1,0:T(8,128)(2,1)S(1)} %collective-permute-done.2.refs_0_), channel_id=1, source_target_pairs={{0,2},{1,3},{2,0},{3,1},{4,6},{5,7},{6,4},{7,5},{8,10},{9,11},{10,... | collective-permute-start | bytes 786440 | tf_op jit(solution)/shard_map/ppermute | solution.py:263
  64.6 1.5 collective-permute-start.8
  66.3 5.0 %collective-permute-done.3.refs_1_ = bf16[2,512,128]{2,1,0:T(8,128)(2,1)} collective-permute-done((bf16[2,512,128]{2,1,0:T(8,128)(2,1)S(1)}, bf16[2,512,128]{2,1,0:T(8,128)(2,1)}, u32[]{:S(2)}, u32[]{:S(2)}) %collective-permute-start.3) | collective-permute-done | bytes 262176 | tf_op jit(solution)/shard_map/ppermute | solution.py:263
  71.3 0.7 copy-done.18
  73.1 5.1 %shard_map.50 = (f32[2,512,512]{2,1,0:T(8,128)}, f32[1,1,128]{2,1,0:T(1,128)}) custom-call(s32[12]{0:T(128)} %stack.77.index_ref, bf16[2,512,128]{2,1,0:T(8,128)(2,1)} %copy-done.5, bf16[2,512,128]{2,1,0:T(8,128)(2,1)} %copy-done.12, bf16[2,512,128]{2,1,0:T(8,128)(2,1)} %copy-done.13, bf16[2,512,128]{2,1,0:T(8,128)(2,1)} %copy-done.15, ...), custom_call_target="tpu_custom_call" | custom-call | flops 536870912 | bytes 4194304 | tf_op jit(solution)/shard_map/pallas_call | solution.py:333
  78.3 5.2 %shard_map.51 = (f32[2,512,512]{2,1,0:T(8,128)}, f32[1,1,128]{2,1,0:T(1,128)}) custom-call(s32[12]{0:T(128)} %stack.77.index_ref, bf16[2,512,128]{2,1,0:T(8,128)(2,1)} %copy-done.14, bf16[2,512,128]{2,1,0:T(8,128)(2,1)} %copy-done.16, bf16[2,512,128]{2,1,0:T(8,128)(2,1)} %copy-done.17, bf16[2,512,128]{2,1,0:T(8,128)(2,1)} %copy-done.18, ...), custom_call_target="tpu_custom_call" | custom-call | flops 536870912 | bytes 4194304 | tf_op jit(solution)/shard_map/pallas_call | solution.py:333
  83.5 5.7 %shard_map.52 = (f32[2,512,512]{2,1,0:T(8,128)}, f32[1,1,128]{2,1,0:T(1,128)}) custom-call(s32[12]{0:T(128)} %stack.77.index_ref, bf16[2,512,128]{2,1,0:T(8,128)(2,1)} %copy-done.19, bf16[2,512,128]{2,1,0:T(8,128)(2,1)} %collective-permute-done.20.refs_1_, bf16[2,512,128]{2,1,0:T(8,128)(2,1)} %copy-done.20, ...), custom_call_target="tpu_custom_call" | custom-call | flops 536870912 | bytes 4194304 | tf_op jit(solution)/shard_map/pallas_call | solution.py:333
  89.3 0.7 copy-done.10
  90.0 6.6 %shard_map.53 = (f32[2,512,512]{2,1,0:T(8,128)}, f32[32,1,128]{2,1,0:T(1,128)}) custom-call(s32[12]{0:T(128)} %stack.77.index_ref, bf16[2,512,128]{2,1,0:T(8,128)(2,1)} %copy-done.11, bf16[2,512,128]{2,1,0:T(8,128)(2,1)} %collective-permute-done.3.refs_1_, bf16[2,512,128]{2,1,0:T(8,128)(2,1)} %collective-permute-done.4.refs_2_, ...), custom_call_target="tpu_custom_call" | custom-call | flops 536870912 | bytes 4194304 | tf_op jit(solution)/shard_map/pallas_call | solution.py:333
  96.6 4.0 %all-to-all-start = ((f32[32,1,128]{2,1,0:T(1,128)}), f32[32,1,128]{2,1,0:T(1,128)S(1)}, u32[]{:S(2)}, u32[]{:S(2)}) async-start(f32[32,1,128]{2,1,0:T(1,128)} %get-tuple-element.21), calls=%async_computation | async-start | bytes 32768 | tf_op jit(solution)/shard_map/all_to_all | solution.py:355
  100.9 1.6 collective-permute-start.26
  102.6 5.2 %all-to-all-done.gram_ref = f32[32,1,128]{2,1,0:T(1,128)S(1)} async-done(((f32[32,1,128]{2,1,0:T(1,128)}), f32[32,1,128]{2,1,0:T(1,128)S(1)}, u32[]{:S(2)}, u32[]{:S(2)}) %all-to-all-start) | async-done | bytes 16416 | tf_op jit(solution)/shard_map/all_to_all | solution.py:355
  108.4 5.5 %combine.1 = (f32[512,512]{1,0:T(8,128)}, f32[1,1]{1,0:T(1,128)}) custom-call(s32[12]{0:T(128)} %stack.77.index_ref, f32[32,1,128]{2,1,0:T(1,128)} %copy-done.21, f32[2,512,512]{2,1,0:T(8,128)} %get-tuple-element.15.refs_6_.refs_0_, f32[2,512,512]{2,1,0:T(8,128)} %get-tuple-element.17.refs_7_.refs_1_, f32[2,512,512]{2,1,0:T(8,128)} %get-tuple-element.19.refs_8_.refs_2_, ...), custom_call_target="tpu_custom_call" | custom-call | flops 4194304 | bytes 8388608 | tf_op jit(solution)/shard_map/combine/pallas_call | solution.py:356
  113.9 2.1 %convert_element_type.102 = f16[512,512]{1,0:T(8,128)(2,1)} convert(f32[512,512]{1,0:T(8,128)} %get-tuple-element.23) | non-fusion elementwise | flops 262144 | bytes 1572864 | tf_op jit(solution)/shard_map/convert_element_type | solution.py:374
  116.6 3.6 %dynamic-slice_bitcast_fusion.2 = (bf16[1024,512]{1,0:T(8,128)(2,1)}, bf16[1024,512]{1,0:T(8,128)(2,1)}, bf16[1024,512]{1,0:T(8,128)(2,1)}) fusion(bf16[4,1024,512]{2,1,0:T(8,128)(2,1)} %bitcast.56, s32[]{:T(128)S(6)} %select_n.108, s32[]{:T(128)S(6)} %select_n.111, s32[]{:T(128)S(6)} %select_n.110), kind=kLoop, calls=%fused_computation.16 | loop fusion | bytes 6291468 | tf_op jit(solution)/shard_map/jit(dynamic_index_in_dim)/squeeze | solution.py:296
  120.8 1.3 collective-permute-start.30
  122.4 9.6 %collective-permute-done.24 = f16[512,512]{1,0:T(8,128)(2,1)} collective-permute-done((f16[512,512]{1,0:T(8,128)(2,1)}, f16[512,512]{1,0:T(8,128)(2,1)}, u32[]{:S(2)}, u32[]{:S(2)}) %collective-permute-start.24) | collective-permute-done | bytes 524320 | tf_op jit(solution)/shard_map/ppermute | solution.py:255
  132.0 2.0 fusion.3
  134.1 1.8 convert_multiply_fusion.7
  135.9 1.0 constant_dynamic-update-slice_fusion.7
  137.0 8.1 %collective-permute-done.27 = f16[512,512]{1,0:T(8,128)(2,1)} collective-permute-done((f16[512,512]{1,0:T(8,128)(2,1)}, f16[512,512]{1,0:T(8,128)(2,1)}, u32[]{:S(2)}, u32[]{:S(2)}) %collective-permute-start.27) | collective-permute-done | bytes 524320 | tf_op jit(solution)/shard_map/ppermute | solution.py:255
  145.5 2.0 fusion.9
  147.5 2.0 fusion.10
  149.4 18.7 %collective-permute-done.30 = bf16[1024,512]{1,0:T(8,128)(2,1)} collective-permute-done((bf16[1024,512]{1,0:T(8,128)(2,1)}, bf16[1024,512]{1,0:T(8,128)(2,1)}, u32[]{:S(2)}, u32[]{:S(2)}) %collective-permute-start.30) | collective-permute-done | bytes 1048608 | tf_op jit(solution)/shard_map/ppermute | solution.py:263
  168.1 2.2 %fusion.2 = bf16[512,1024]{0,1:T(8,128)(2,1)S(1)} fusion(f32[512,1024]{0,1:T(8,128)S(1)} %fusion.10, f32[512,1024]{0,1:T(8,128)S(1)} %fusion.9, f32[1024,512]{1,0:T(8,128)S(1)} %fusion.3, bf16[512,512]{1,0:T(8,128)(2,1)} %collective-permute-done.29, bf16[1024,512]{1,0:T(8,128)(2,1)} %collective-permute-done.30), kind=kOutput, calls=%fused_computation.3 | convolution fusion | flops 538968064 | bytes 8912896 | tf_op jit(solution)/shard_map/dot_general | solution.py:387
  170.3 1.3 copy.8
  171.7 1.8 convert_multiply_fusion.6
  174.6 1.5 collective-permute-start.34
  176.1 1.8 convert_multiply_fusion.5
  177.9 1.0 constant_dynamic-update-slice_fusion.6
  179.0 1.0 constant_dynamic-update-slice_fusion.5
  180.0 1.8 convert_multiply_fusion.3
  181.8 7.8 %collective-permute-done.31 = f16[512,512]{1,0:T(8,128)(2,1)S(1)} collective-permute-done((f16[512,512]{1,0:T(8,128)(2,1)}, f16[512,512]{1,0:T(8,128)(2,1)S(1)}, u32[]{:S(2)}, u32[]{:S(2)}) %collective-permute-start.31) | collective-permute-done | bytes 524320 | tf_op jit(solution)/shard_map/ppermute | solution.py:255
  190.2 0.7 convert_multiply_fusion.4
  191.0 1.0 constant_dynamic-update-slice_fusion.4
  192.0 1.0 constant_dynamic-update-slice_fusion.3
  193.1 0.7 convert_multiply_fusion.2
  193.8 1.0 constant_dynamic-update-slice_fusion.2
  194.9 5.5 %collective-permute-done.34 = f16[512,512]{1,0:T(8,128)(2,1)S(1)} collective-permute-done((f16[512,512]{1,0:T(8,128)(2,1)}, f16[512,512]{1,0:T(8,128)(2,1)S(1)}, u32[]{:S(2)}, u32[]{:S(2)}) %collective-permute-start.34) | collective-permute-done | bytes 524320 | tf_op jit(solution)/shard_map/ppermute | solution.py:259
  200.3 0.7 convert_multiply_fusion.1
  201.1 1.0 constant_dynamic-update-slice_fusion.1
  202.1 8.5 %collective-permute-done.35 = f16[512,512]{1,0:T(8,128)(2,1)S(1)} collective-permute-done((f16[512,512]{1,0:T(8,128)(2,1)S(1)}, f16[512,512]{1,0:T(8,128)(2,1)S(1)}, u32[]{:S(2)}, u32[]{:S(2)}) %collective-permute-start.35) | collective-permute-done | bytes 524320 | tf_op jit(solution)/shard_map/ppermute | solution.py:259
  210.6 0.7 convert_multiply_fusion
  211.4 1.0 constant_dynamic-update-slice_fusion
  (93 shorter events, 7.0 us)
Async XLA Ops:
  0.7 1.2 copy-start
  2.8 15.8 %collective-permute-start.1 = (bf16[4,512,128]{2,1,0:T(8,128)(2,1)S(1)}, bf16[4,512,128]{2,1,0:T(8,128)(2,1)S(1)}, u32[]{:S(2)}, u32[]{:S(2)}) collective-permute-start(bf16[4,512,128]{2,1,0:T(8,128)(2,1)S(1)} %pack.3), channel_id=1, source_target_pairs={{0,4},{4,0},{8,12},{12,8},{16,20},{20,16},{24,28},{28,24},{1,5},{5... | collective-permute-start | bytes 1572872 | tf_op jit(solution)/shard_map/ppermute | solution.py:259
  5.9 23.2 %collective-permute-start.12 = (bf16[512,512]{1,0:T(8,128)(2,1)}, bf16[512,512]{1,0:T(8,128)(2,1)S(1)}, u32[]{:S(2)}, u32[]{:S(2)}) collective-permute-start(bf16[512,512]{1,0:T(8,128)(2,1)} %refs_4_.1), channel_id=1, source_target_pairs={{0,4},{4,0},{8,12},{12,8},{16,20},{20,16},{24,28},{28,24},{1,5},{5... | collective-permute-start | bytes 1572872 | tf_op jit(solution)/shard_map/ppermute | solution.py:259
  6.0 24.9 %collective-permute-start.17 = (bf16[512,512]{1,0:T(8,128)(2,1)}, bf16[512,512]{1,0:T(8,128)(2,1)S(1)}, u32[]{:S(2)}, u32[]{:S(2)}) collective-permute-start(bf16[512,512]{1,0:T(8,128)(2,1)} %refs_4_.1), channel_id=1, source_target_pairs={{0,8},{4,12},{8,0},{12,4},{16,24},{20,28},{24,16},{28,20},{1,9},{5... | collective-permute-start | bytes 1572872 | tf_op jit(solution)/shard_map/ppermute | solution.py:255
  8.0 25.6 %collective-permute-start.6 = (bf16[512,512]{1,0:T(8,128)(2,1)}, bf16[512,512]{1,0:T(8,128)(2,1)}, u32[]{:S(2)}, u32[]{:S(2)}) collective-permute-start(bf16[512,512]{1,0:T(8,128)(2,1)} %refs_4_.1), channel_id=1, source_target_pairs={{0,16},{4,20},{8,24},{12,28},{16,0},{20,4},{24,8},{28,12},{1,17},{... | collective-permute-start | bytes 1572872 | tf_op jit(solution)/shard_map/ppermute | solution.py:255
  10.6 1.2 copy-start.1
  18.7 54.4 %copy-start.5 = (bf16[2,512,128]{2,1,0:T(8,128)(2,1)}, bf16[2,512,128]{2,1,0:T(8,128)(2,1)S(1)}, u32[]{:S(2)}) copy-start(bf16[2,512,128]{2,1,0:T(8,128)(2,1)S(1)} %pad_maximum_fusion.1.refs_0_) | copy-start | bytes 786436
  18.7 17.1 %collective-permute-start.9 = (bf16[2,512,128]{2,1,0:T(8,128)(2,1)S(1)}, bf16[2,512,128]{2,1,0:T(8,128)(2,1)S(1)}, u32[]{:S(2)}, u32[]{:S(2)}) collective-permute-start(bf16[2,512,128]{2,1,0:T(8,128)(2,1)S(1)} %pad_maximum_fusion.1.refs_0_), channel_id=1, source_target_pairs={{0,2},{1,3},{2,0},{3,1},{4,6},{5,7},{6,4},{7,5},{8,10},{9,11},{10,... | collective-permute-start | bytes 786440 | tf_op jit(solution)/shard_map/ppermute | solution.py:263
  20.8 16.6 %collective-permute-start.10 = (bf16[2,512,128]{2,1,0:T(8,128)(2,1)S(1)}, bf16[2,512,128]{2,1,0:T(8,128)(2,1)S(1)}, u32[]{:S(2)}, u32[]{:S(2)}) collective-permute-start(bf16[2,512,128]{2,1,0:T(8,128)(2,1)S(1)} %pad_maximum_fusion.1.refs_0_), channel_id=1, source_target_pairs={{0,1},{1,0},{2,3},{3,2},{4,5},{5,4},{6,7},{7,6},{8,9},{9,8},{10,11... | collective-permute-start | bytes 786440 | tf_op jit(solution)/shard_map/ppermute | solution.py:263
  29.0 44.1 %copy-start.7 = (bf16[512,512]{1,0:T(8,128)(2,1)}, bf16[512,512]{1,0:T(8,128)(2,1)S(1)}, u32[]{:S(2)}) copy-start(bf16[512,512]{1,0:T(8,128)(2,1)S(1)} %collective-permute-done.12.refs_5_) | copy-start | bytes 1572868
  29.0 12.2 %collective-permute-start.13 = (bf16[2,512,128]{2,1,0:T(8,128)(2,1)S(1)}, bf16[2,512,128]{2,1,0:T(8,128)(2,1)S(1)}, u32[]{:S(2)}, u32[]{:S(2)}) collective-permute-start(bf16[2,512,128]{2,1,0:T(8,128)(2,1)S(1)} %pad_maximum_fusion.2), channel_id=1, source_target_pairs={{0,8},{4,12},{8,0},{12,4},{16,24},{20,28},{24,16},{28,20},{1,9},{5... | collective-permute-start | bytes 786440 | tf_op jit(solution)/shard_map/ppermute | solution.py:255
  30.9 47.4 %copy-start.6 = (bf16[512,512]{1,0:T(8,128)(2,1)}, bf16[512,512]{1,0:T(8,128)(2,1)S(1)}, u32[]{:S(2)}) copy-start(bf16[512,512]{1,0:T(8,128)(2,1)S(1)} %collective-permute-done.17.refs_4_) | copy-start | bytes 1572868
  30.9 21.4 %collective-permute-start.19 = (bf16[2,512,128]{2,1,0:T(8,128)(2,1)S(1)}, bf16[2,512,128]{2,1,0:T(8,128)(2,1)S(1)}, u32[]{:S(2)}, u32[]{:S(2)}) collective-permute-start(bf16[2,512,128]{2,1,0:T(8,128)(2,1)S(1)} %pad_maximum_fusion.3), channel_id=1, source_target_pairs={{0,16},{4,20},{8,24},{12,28},{16,0},{20,4},{24,8},{28,12},{1,17},{... | collective-permute-start | bytes 786440 | tf_op jit(solution)/shard_map/ppermute | solution.py:255
  33.6 20.3 %collective-permute-start.2 = (bf16[2,512,128]{2,1,0:T(8,128)(2,1)S(1)}, bf16[2,512,128]{2,1,0:T(8,128)(2,1)S(1)}, u32[]{:S(2)}, u32[]{:S(2)}) collective-permute-start(bf16[2,512,128]{2,1,0:T(8,128)(2,1)S(1)} %pad_maximum_fusion), channel_id=1, source_target_pairs={{0,24},{4,28},{8,16},{12,20},{16,8},{20,12},{24,0},{28,4},{1,25},{... | collective-permute-start | bytes 786440 | tf_op jit(solution)/shard_map/ppermute | solution.py:255
  35.9 37.3 %copy-start.12 = (bf16[2,512,128]{2,1,0:T(8,128)(2,1)}, bf16[2,512,128]{2,1,0:T(8,128)(2,1)S(1)}, u32[]{:S(2)}) copy-start(bf16[2,512,128]{2,1,0:T(8,128)(2,1)S(1)} %collective-permute-done.9.refs_1_) | copy-start | bytes 786436
  35.9 26.2 %collective-permute-start.18 = (bf16[512,512]{1,0:T(8,128)(2,1)S(1)}, bf16[512,512]{1,0:T(8,128)(2,1)S(1)}, u32[]{:S(2)}, u32[]{:S(2)}) collective-permute-start(bf16[512,512]{1,0:T(8,128)(2,1)S(1)} %collective-permute-done.17.refs_4_), channel_id=1, source_target_pairs={{0,4},{4,0},{8,12},{12,8},{16,20},{20,16},{24,28},{28,24},{1,5},{5... | collective-permute-start | bytes 1572872 | tf_op jit(solution)/shard_map/ppermute | solution.py:259
  37.4 0.7 copy-start.13
  37.4 16.5 %collective-permute-start.11 = (bf16[2,512,128]{2,1,0:T(8,128)(2,1)S(1)}, bf16[2,512,128]{2,1,0:T(8,128)(2,1)S(1)}, u32[]{:S(2)}, u32[]{:S(2)}) collective-permute-start(bf16[2,512,128]{2,1,0:T(8,128)(2,1)S(1)} %collective-permute-done.9.refs_1_), channel_id=1, source_target_pairs={{0,1},{1,0},{2,3},{3,2},{4,5},{5,4},{6,7},{7,6},{8,9},{9,8},{10,11... | collective-permute-start | bytes 786440 | tf_op jit(solution)/shard_map/ppermute | solution.py:263
  41.2 23.4 %copy-start.14 = (bf16[2,512,128]{2,1,0:T(8,128)(2,1)}, bf16[2,512,128]{2,1,0:T(8,128)(2,1)S(1)}, u32[]{:S(2)}) copy-start(bf16[2,512,128]{2,1,0:T(8,128)(2,1)S(1)} %collective-permute-done.13.refs_0_) | copy-start | bytes 786436
  41.2 23.4 %collective-permute-start.7 = (bf16[512,512]{1,0:T(8,128)(2,1)}, bf16[512,512]{1,0:T(8,128)(2,1)S(1)}, u32[]{:S(2)}, u32[]{:S(2)}) collective-permute-start(bf16[512,512]{1,0:T(8,128)(2,1)} %collective-permute-done.6.refs_4_), channel_id=1, source_target_pairs={{0,8},{4,12},{8,0},{12,4},{16,24},{20,28},{24,16},{28,20},{1,9},{5... | collective-permute-start | bytes 1572872 | tf_op jit(solution)/shard_map/ppermute | solution.py:255
  52.3 18.9 %copy-start.19 = (bf16[2,512,128]{2,1,0:T(8,128)(2,1)}, bf16[2,512,128]{2,1,0:T(8,128)(2,1)S(1)}, u32[]{:S(2)}) copy-start(bf16[2,512,128]{2,1,0:T(8,128)(2,1)S(1)} %collective-permute-done.19.refs_0_) | copy-start | bytes 786436
  52.3 8.1 %collective-permute-start.14 = (bf16[2,512,128]{2,1,0:T(8,128)(2,1)S(1)}, bf16[2,512,128]{2,1,0:T(8,128)(2,1)S(1)}, u32[]{:S(2)}, u32[]{:S(2)}) collective-permute-start(bf16[2,512,128]{2,1,0:T(8,128)(2,1)S(1)} %collective-permute-done.13.refs_0_), channel_id=1, source_target_pairs={{0,2},{1,3},{2,0},{3,1},{4,6},{5,7},{6,4},{7,5},{8,10},{9,11},{10,... | collective-permute-start | bytes 786440 | tf_op jit(solution)/shard_map/ppermute | solution.py:263
  53.8 35.4 %copy-start.11 = (bf16[2,512,128]{2,1,0:T(8,128)(2,1)}, bf16[2,512,128]{2,1,0:T(8,128)(2,1)S(1)}, u32[]{:S(2)}) copy-start(bf16[2,512,128]{2,1,0:T(8,128)(2,1)S(1)} %collective-permute-done.2.refs_0_) | copy-start | bytes 786436
  53.8 6.6 %collective-permute-start.15 = (bf16[2,512,128]{2,1,0:T(8,128)(2,1)S(1)}, bf16[2,512,128]{2,1,0:T(8,128)(2,1)S(1)}, u32[]{:S(2)}, u32[]{:S(2)}) collective-permute-start(bf16[2,512,128]{2,1,0:T(8,128)(2,1)S(1)} %collective-permute-done.13.refs_0_), channel_id=1, source_target_pairs={{0,1},{1,0},{2,3},{3,2},{4,5},{5,4},{6,7},{7,6},{8,9},{9,8},{10,11... | collective-permute-start | bytes 786440 | tf_op jit(solution)/shard_map/ppermute | solution.py:263
  53.9 10.7 %copy-start.15 = (bf16[2,512,128]{2,1,0:T(8,128)(2,1)}, bf16[2,512,128]{2,1,0:T(8,128)(2,1)S(1)}, u32[]{:S(2)}) copy-start(bf16[2,512,128]{2,1,0:T(8,128)(2,1)S(1)} %collective-permute-done.11.refs_3_) | copy-start | bytes 786436
  53.9 10.7 %collective-permute-start.20 = (bf16[2,512,128]{2,1,0:T(8,128)(2,1)S(1)}, bf16[2,512,128]{2,1,0:T(8,128)(2,1)}, u32[]{:S(2)}, u32[]{:S(2)}) collective-permute-start(bf16[2,512,128]{2,1,0:T(8,128)(2,1)S(1)} %collective-permute-done.19.refs_0_), channel_id=1, source_target_pairs={{0,2},{1,3},{2,0},{3,1},{4,6},{5,7},{6,4},{7,5},{8,10},{9,11},{10,... | collective-permute-start | bytes 786440 | tf_op jit(solution)/shard_map/ppermute | solution.py:263
  60.5 10.8 %copy-start.16 = (bf16[2,512,128]{2,1,0:T(8,128)(2,1)}, bf16[2,512,128]{2,1,0:T(8,128)(2,1)S(1)}, u32[]{:S(2)}) copy-start(bf16[2,512,128]{2,1,0:T(8,128)(2,1)S(1)} %collective-permute-done.14.refs_1_) | copy-start | bytes 786436
  60.5 5.6 %collective-permute-start.21 = (bf16[2,512,128]{2,1,0:T(8,128)(2,1)S(1)}, bf16[2,512,128]{2,1,0:T(8,128)(2,1)S(1)}, u32[]{:S(2)}, u32[]{:S(2)}) collective-permute-start(bf16[2,512,128]{2,1,0:T(8,128)(2,1)S(1)} %collective-permute-done.19.refs_0_), channel_id=1, source_target_pairs={{0,1},{1,0},{2,3},{3,2},{4,5},{5,4},{6,7},{7,6},{8,9},{9,8},{10,11... | collective-permute-start | bytes 786440 | tf_op jit(solution)/shard_map/ppermute | solution.py:263
  60.5 10.8 %copy-start.17 = (bf16[2,512,128]{2,1,0:T(8,128)(2,1)}, bf16[2,512,128]{2,1,0:T(8,128)(2,1)S(1)}, u32[]{:S(2)}) copy-start(bf16[2,512,128]{2,1,0:T(8,128)(2,1)S(1)} %collective-permute-done.15.refs_2_) | copy-start | bytes 786436
  60.5 23.0 %collective-permute-start.23 = (bf16[512,512]{1,0:T(8,128)(2,1)}, bf16[512,512]{1,0:T(8,128)(2,1)}, u32[]{:S(2)}, u32[]{:S(2)}) collective-permute-start(bf16[512,512]{1,0:T(8,128)(2,1)} %collective-permute-done.6.refs_4_), channel_id=1, source_target_pairs={{0,4},{4,0},{8,12},{12,8},{16,20},{20,16},{24,28},{28,24},{1,5},{5... | collective-permute-start | bytes 1572872 | tf_op jit(solution)/shard_map/ppermute | solution.py:259
  62.1 16.2 %copy-start.9 = (bf16[512,512]{1,0:T(8,128)(2,1)}, bf16[512,512]{1,0:T(8,128)(2,1)S(1)}, u32[]{:S(2)}) copy-start(bf16[512,512]{1,0:T(8,128)(2,1)S(1)} %collective-permute-done.18.refs_5_) | copy-start | bytes 1572868
  62.1 9.2 %collective-permute-start.3 = (bf16[2,512,128]{2,1,0:T(8,128)(2,1)S(1)}, bf16[2,512,128]{2,1,0:T(8,128)(2,1)}, u32[]{:S(2)}, u32[]{:S(2)}) collective-permute-start(bf16[2,512,128]{2,1,0:T(8,128)(2,1)S(1)} %collective-permute-done.2.refs_0_), channel_id=1, source_target_pairs={{0,2},{1,3},{2,0},{3,1},{4,6},{5,7},{6,4},{7,5},{8,10},{9,11},{10,... | collective-permute-start | bytes 786440 | tf_op jit(solution)/shard_map/ppermute | solution.py:263
  64.5 6.7 %collective-permute-start.16 = (bf16[2,512,128]{2,1,0:T(8,128)(2,1)S(1)}, bf16[2,512,128]{2,1,0:T(8,128)(2,1)S(1)}, u32[]{:S(2)}, u32[]{:S(2)}) collective-permute-start(bf16[2,512,128]{2,1,0:T(8,128)(2,1)S(1)} %collective-permute-done.14.refs_1_), channel_id=1, source_target_pairs={{0,1},{1,0},{2,3},{3,2},{4,5},{5,4},{6,7},{7,6},{8,9},{9,8},{10,11... | collective-permute-start | bytes 786440 | tf_op jit(solution)/shard_map/ppermute | solution.py:263
  64.6 24.7 %copy-start.8 = (bf16[512,512]{1,0:T(8,128)(2,1)}, bf16[512,512]{1,0:T(8,128)(2,1)S(1)}, u32[]{:S(2)}) copy-start(bf16[512,512]{1,0:T(8,128)(2,1)S(1)} %collective-permute-done.7.refs_4_) | copy-start | bytes 1572868
  64.6 24.7 %collective-permute-start.8 = (bf16[512,512]{1,0:T(8,128)(2,1)S(1)}, bf16[512,512]{1,0:T(8,128)(2,1)S(1)}, u32[]{:S(2)}, u32[]{:S(2)}) collective-permute-start(bf16[512,512]{1,0:T(8,128)(2,1)S(1)} %collective-permute-done.7.refs_4_), channel_id=1, source_target_pairs={{0,4},{4,0},{8,12},{12,8},{16,20},{20,16},{24,28},{28,24},{1,5},{5... | collective-permute-start | bytes 1572872 | tf_op jit(solution)/shard_map/ppermute | solution.py:259
  66.1 5.2 %copy-start.20 = (bf16[2,512,128]{2,1,0:T(8,128)(2,1)}, bf16[2,512,128]{2,1,0:T(8,128)(2,1)S(1)}, u32[]{:S(2)}) copy-start(bf16[2,512,128]{2,1,0:T(8,128)(2,1)S(1)} %collective-permute-done.21.refs_2_) | copy-start | bytes 786436
  66.1 17.5 %collective-permute-start.22 = (bf16[2,512,128]{2,1,0:T(8,128)(2,1)}, bf16[2,512,128]{2,1,0:T(8,128)(2,1)}, u32[]{:S(2)}, u32[]{:S(2)}) collective-permute-start(bf16[2,512,128]{2,1,0:T(8,128)(2,1)} %collective-permute-done.20.refs_1_), channel_id=1, source_target_pairs={{0,1},{1,0},{2,3},{3,2},{4,5},{5,4},{6,7},{7,6},{8,9},{9,8},{10,11... | collective-permute-start | bytes 786440 | tf_op jit(solution)/shard_map/ppermute | solution.py:263
  71.3 18.0 %collective-permute-start.4 = (bf16[2,512,128]{2,1,0:T(8,128)(2,1)S(1)}, bf16[2,512,128]{2,1,0:T(8,128)(2,1)}, u32[]{:S(2)}, u32[]{:S(2)}) collective-permute-start(bf16[2,512,128]{2,1,0:T(8,128)(2,1)S(1)} %collective-permute-done.2.refs_0_), channel_id=1, source_target_pairs={{0,1},{1,0},{2,3},{3,2},{4,5},{5,4},{6,7},{7,6},{8,9},{9,8},{10,11... | collective-permute-start | bytes 786440 | tf_op jit(solution)/shard_map/ppermute | solution.py:263
  71.3 0.7 copy-start.18
  72.0 17.2 %collective-permute-start.5 = (bf16[2,512,128]{2,1,0:T(8,128)(2,1)}, bf16[2,512,128]{2,1,0:T(8,128)(2,1)}, u32[]{:S(2)}, u32[]{:S(2)}) collective-permute-start(bf16[2,512,128]{2,1,0:T(8,128)(2,1)} %collective-permute-done.3.refs_1_), channel_id=1, source_target_pairs={{0,1},{1,0},{2,3},{3,2},{4,5},{5,4},{6,7},{7,6},{8,9},{9,8},{10,11... | collective-permute-start | bytes 786440 | tf_op jit(solution)/shard_map/ppermute | solution.py:263
  83.5 17.1 %copy-start.2 = (bf16[512,512]{1,0:T(8,128)(2,1)S(1)}, bf16[512,512]{1,0:T(8,128)(2,1)}, u32[]{:S(2)}) copy-start(bf16[512,512]{1,0:T(8,128)(2,1)} %refs_4_.1) | copy-start | bytes 1572868
  89.3 0.8 copy-start.10
  96.6 11.2 %all-to-all-start = ((f32[32,1,128]{2,1,0:T(1,128)}), f32[32,1,128]{2,1,0:T(1,128)S(1)}, u32[]{:S(2)}, u32[]{:S(2)}) async-start(f32[32,1,128]{2,1,0:T(1,128)} %get-tuple-element.21), calls=%async_computation | async-start | bytes 32768 | tf_op jit(solution)/shard_map/all_to_all | solution.py:355
  100.6 20.2 %collective-permute-start = (bf16[512,512]{1,0:T(8,128)(2,1)S(1)}, bf16[512,512]{1,0:T(8,128)(2,1)S(1)}, u32[]{:S(2)}, u32[]{:S(2)}) collective-permute-start(bf16[512,512]{1,0:T(8,128)(2,1)S(1)} %copy-done.2), channel_id=1, source_target_pairs={{0,1},{1,0},{2,3},{3,2},{4,5},{5,4},{6,7},{7,6},{8,9},{9,8},{10,11... | collective-permute-start | bytes 1572872 | tf_op jit(solution)/shard_map/ppermute | solution.py:263
  100.9 21.2 %collective-permute-start.26 = (bf16[512,512]{1,0:T(8,128)(2,1)S(1)}, bf16[512,512]{1,0:T(8,128)(2,1)S(1)}, u32[]{:S(2)}, u32[]{:S(2)}) collective-permute-start(bf16[512,512]{1,0:T(8,128)(2,1)S(1)} %copy-done.2), channel_id=1, source_target_pairs={{0,2},{1,3},{2,0},{3,1},{4,6},{5,7},{6,4},{7,5},{8,10},{9,11},{10,... | collective-permute-start | bytes 1572872 | tf_op jit(solution)/shard_map/ppermute | solution.py:263
  107.8 0.6 copy-start.21
  116.1 15.9 %collective-permute-start.24 = (f16[512,512]{1,0:T(8,128)(2,1)}, f16[512,512]{1,0:T(8,128)(2,1)}, u32[]{:S(2)}, u32[]{:S(2)}) collective-permute-start(f16[512,512]{1,0:T(8,128)(2,1)} %convert_element_type.102), channel_id=1, source_target_pairs={{0,8},{4,12},{8,16},{12,20},{16,24},{20,28},{24,0},{28,4},{1,9},{5... | collective-permute-start | bytes 1572872 | tf_op jit(solution)/shard_map/ppermute | solution.py:255
  120.2 25.3 %collective-permute-start.25 = (bf16[1024,512]{1,0:T(8,128)(2,1)}, bf16[1024,512]{1,0:T(8,128)(2,1)}, u32[]{:S(2)}, u32[]{:S(2)}) collective-permute-start(bf16[1024,512]{1,0:T(8,128)(2,1)} %get-tuple-element.30), channel_id=1, source_target_pairs={{0,1},{1,0},{2,3},{3,2},{4,5},{5,4},{6,7},{7,6},{8,9},{9,8},{10,11... | collective-permute-start | bytes 3145736 | tf_op jit(solution)/shard_map/ppermute | solution.py:263
  120.2 27.2 %collective-permute-start.28 = (bf16[1024,512]{1,0:T(8,128)(2,1)}, bf16[1024,512]{1,0:T(8,128)(2,1)}, u32[]{:S(2)}, u32[]{:S(2)}) collective-permute-start(bf16[1024,512]{1,0:T(8,128)(2,1)} %get-tuple-element.32), channel_id=1, source_target_pairs={{0,2},{1,3},{2,0},{3,1},{4,6},{5,7},{6,4},{7,5},{8,10},{9,11},{10,... | collective-permute-start | bytes 3145736 | tf_op jit(solution)/shard_map/ppermute | solution.py:263
  120.8 11.2 %copy-start.3 = (bf16[512,512]{1,0:T(8,128)(2,1)}, bf16[512,512]{1,0:T(8,128)(2,1)S(1)}, u32[]{:S(2)}) copy-start(bf16[512,512]{1,0:T(8,128)(2,1)S(1)} %collective-permute-done) | copy-start | bytes 1572868
  120.8 47.4 %collective-permute-start.30 = (bf16[1024,512]{1,0:T(8,128)(2,1)}, bf16[1024,512]{1,0:T(8,128)(2,1)}, u32[]{:S(2)}, u32[]{:S(2)}) collective-permute-start(bf16[1024,512]{1,0:T(8,128)(2,1)} %get-tuple-element.31), channel_id=1, source_target_pairs={{0,3},{1,2},{2,1},{3,0},{4,7},{5,6},{6,5},{7,4},{8,11},{9,10},{10,... | collective-permute-start | bytes 3145736 | tf_op jit(solution)/shard_map/ppermute | solution.py:263
  122.1 23.4 %collective-permute-start.29 = (bf16[512,512]{1,0:T(8,128)(2,1)S(1)}, bf16[512,512]{1,0:T(8,128)(2,1)}, u32[]{:S(2)}, u32[]{:S(2)}) collective-permute-start(bf16[512,512]{1,0:T(8,128)(2,1)S(1)} %collective-permute-done.26), channel_id=1, source_target_pairs={{0,1},{1,0},{2,3},{3,2},{4,5},{5,4},{6,7},{7,6},{8,9},{9,8},{10,11... | collective-permute-start | bytes 1572872 | tf_op jit(solution)/shard_map/ppermute | solution.py:263
  132.0 13.1 %collective-permute-start.27 = (f16[512,512]{1,0:T(8,128)(2,1)}, f16[512,512]{1,0:T(8,128)(2,1)}, u32[]{:S(2)}, u32[]{:S(2)}) collective-permute-start(f16[512,512]{1,0:T(8,128)(2,1)} %convert_element_type.102), channel_id=1, source_target_pairs={{0,24},{4,28},{8,0},{12,4},{16,8},{20,12},{24,16},{28,20},{1,25},{... | collective-permute-start | bytes 1572872 | tf_op jit(solution)/shard_map/ppermute | solution.py:255
  133.9 11.6 %copy-start.4 = (bf16[512,512]{1,0:T(8,128)(2,1)S(1)}, bf16[512,512]{1,0:T(8,128)(2,1)}, u32[]{:S(2)}) copy-start(bf16[512,512]{1,0:T(8,128)(2,1)} %copy-done.3) | copy-start | bytes 1572868
  145.0 35.0 %collective-permute-start.32 = (f16[512,512]{1,0:T(8,128)(2,1)}, f16[512,512]{1,0:T(8,128)(2,1)}, u32[]{:S(2)}, u32[]{:S(2)}) collective-permute-start(f16[512,512]{1,0:T(8,128)(2,1)} %convert_element_type.102), channel_id=1, source_target_pairs={{0,4},{4,0},{8,12},{12,8},{16,20},{20,16},{24,28},{28,24},{1,5},{5... | collective-permute-start | bytes 1572872 | tf_op jit(solution)/shard_map/ppermute | solution.py:259
  173.5 16.2 %collective-permute-start.31 = (f16[512,512]{1,0:T(8,128)(2,1)}, f16[512,512]{1,0:T(8,128)(2,1)S(1)}, u32[]{:S(2)}, u32[]{:S(2)}) collective-permute-start(f16[512,512]{1,0:T(8,128)(2,1)} %collective-permute-done.24), channel_id=1, source_target_pairs={{0,8},{4,12},{8,16},{12,20},{16,24},{20,28},{24,0},{28,4},{1,9},{5... | collective-permute-start | bytes 1572872 | tf_op jit(solution)/shard_map/ppermute | solution.py:255
  174.1 19.0 %collective-permute-start.33 = (f16[512,512]{1,0:T(8,128)(2,1)}, f16[512,512]{1,0:T(8,128)(2,1)S(1)}, u32[]{:S(2)}, u32[]{:S(2)}) collective-permute-start(f16[512,512]{1,0:T(8,128)(2,1)} %collective-permute-done.24), channel_id=1, source_target_pairs={{0,4},{4,0},{8,12},{12,8},{16,20},{20,16},{24,28},{28,24},{1,5},{5... | collective-permute-start | bytes 1572872 | tf_op jit(solution)/shard_map/ppermute | solution.py:259
  174.6 25.7 %collective-permute-start.34 = (f16[512,512]{1,0:T(8,128)(2,1)}, f16[512,512]{1,0:T(8,128)(2,1)S(1)}, u32[]{:S(2)}, u32[]{:S(2)}) collective-permute-start(f16[512,512]{1,0:T(8,128)(2,1)} %collective-permute-done.27), channel_id=1, source_target_pairs={{0,4},{4,0},{8,12},{12,8},{16,20},{20,16},{24,28},{28,24},{1,5},{5... | collective-permute-start | bytes 1572872 | tf_op jit(solution)/shard_map/ppermute | solution.py:259
  189.6 21.0 %collective-permute-start.35 = (f16[512,512]{1,0:T(8,128)(2,1)S(1)}, f16[512,512]{1,0:T(8,128)(2,1)S(1)}, u32[]{:S(2)}, u32[]{:S(2)}) collective-permute-start(f16[512,512]{1,0:T(8,128)(2,1)S(1)} %collective-permute-done.31), channel_id=1, source_target_pairs={{0,4},{4,0},{8,12},{12,8},{16,20},{20,16},{24,28},{28,24},{1,5},{5... | collective-permute-start | bytes 1572872 | tf_op jit(solution)/shard_map/ppermute | solution.py:259

commit v2 on v1

--- a/solution.py
+++ b/solution.py
@@ -105,27 +105,24 @@
     earlier, refs = refs[:lines], refs[lines:]
     total_ref, refs = (refs[0], refs[1:]) if lines else (None, refs)
     grads_ref, gram_ref, acts, cotangents, held, sems = refs
-    width, columns = acts.shape[3], cotangents.shape[2]
+    width, columns = acts.shape[1] // groups, cotangents.shape[2]
     count = index_ref.shape[0] - groups
     features = groups * width
     loads = fetch(
         [(cots[l], cotangents.at[l]) for l in range(replicas)]
-        + [(slices[m], acts.at[m]) for m in range(groups)]
+        + [(slices[m], acts.at[:, pl.ds(m * width, width), :]) for m in range(groups)]
         + [(earlier[i], held.at[i]) for i in range(lines)],
         sems,
     )
-    for copy in loads[:replicas]:
+    for copy in loads[: replicas + groups]:
         copy.wait()
-    for m in range(groups):
-        loads[replicas + m].wait()
-        for l in range(replicas):
+    for l in range(replicas):
+        block = lax.dot_general(
+            acts[l], cotangents[l], (((1,), (0,)), ((), ())), preferred_element_type=jnp.float32
+        )
+        for m in range(groups):
             at = pl.multiple_of(index_ref[m] * width, width)
-            held[lines, l, pl.ds(at, width), :] = lax.dot_general(
-                acts[m, l],
-                cotangents[l],
-                (((0,), (0,)), ((), ())),
-                preferred_element_type=jnp.float32,
-            )
+            held[lines, l, pl.ds(at, width), :] = block[m * width : (m + 1) * width]
     store = pltpu.make_async_copy(held.at[lines], grads_ref, sems.at[len(loads)])
     store.start()
     for copy in loads[groups + replicas :]:
@@ -206,7 +203,7 @@
 
 
 def pack_kernel(index_ref, attention_ref, packed_ref):
-    packed_ref[...] = attention_ref[...].reshape(packed_ref.shape)
+    packed_ref[0] = attention_ref[...].T
 
 
 def pack(index, attention, width):
@@ -217,9 +214,9 @@
             num_scalar_prefetch=1,
             grid=(index.shape[0],),
             in_specs=[pl.BlockSpec((rows, width), lambda i, index: (0, index[i]))],
-            out_specs=pl.BlockSpec((1, rows, width), lambda i, index: (i, 0, 0)),
+            out_specs=pl.BlockSpec((1, width, rows), lambda i, index: (i, 0, 0)),
         ),
-        out_shape=jax.ShapeDtypeStruct((index.shape[0], rows, width), attention.dtype),
+        out_shape=jax.ShapeDtypeStruct((index.shape[0], width, rows), attention.dtype),
         compiler_params=pltpu.CompilerParams(vmem_limit_bytes=4 * 2**20),
         name="pack",
     )(index, attention)
@@ -339,7 +336,7 @@
                 jax.ShapeDtypeStruct((copies, 1, lanes), jnp.float32),
             ),
             scratch_shapes=[
-                pltpu.VMEM((groups, inner, rows, width), attention.dtype),
+                pltpu.VMEM((inner, features, rows), attention.dtype),
                 pltpu.VMEM((inner, rows, columns), cotangent.dtype),
                 pltpu.VMEM((at + 1, inner, features, columns), jnp.float32),
                 pltpu.SemaphoreType.DMA((len(operands) + 1,)),
@@ -353,6 +350,17 @@
         grads.append(block)
 
     shared = lax.all_to_all(gram, ("dp", "tensor"), 0, 0, tiled=True).reshape(n * groups, 1, lanes)
+
+    def input_term(key, *others):
+        return lax.dot_general(
+            after(cot_blocks[key], *others),
+            row_blocks[key],
+            (((1,), (1,)), ((), ())),
+            preferred_element_type=jnp.float32,
+        )
+
+    total = input_term((0, 0), gram) + input_term((0, 1), gram)
+    shared = after(shared, total)
     sent, scale = pl.pallas_call(
         functools.partial(combine_kernel, inner, groups),
         in_specs=[smem, pl.BlockSpec(memory_space=pltpu.VMEM)] + [hbm] * outer,
@@ -372,20 +380,22 @@
     )(index, shared, *grads)
     combined = unwritten((groups, n, width, columns))
     lines = by_ring(after(sent.astype(jnp.float16)))
-    for l in range(inner):
-        for k in ring_order:
-            values = lines[k][l].reshape(groups, 1, width, columns).astype(jnp.float32) * scale[0, 0]
+    half = outer // 2
+    for l in range(1, inner):
+        first, second = lines[half][0][: features // 2], lines[half - 1][l][features // 2 :]
+        lines[half][l] = [along_y(first, l), along_z(second, lambda i: (i + 1) % outer)]
+    for k in ring_order:
+        for l in range(inner):
             source = (z - k) % outer * inner + (y ^ l)
-            combined = lax.dynamic_update_slice_in_dim(combined, values, source, 1)
+            parts = lines[k][l] if isinstance(lines[k][l], list) else [lines[k][l]]
+            for at, block in enumerate(parts):
+                share = groups // len(parts)
+                values = block.reshape(share, 1, width, columns).astype(jnp.float32) * scale[0, 0]
+                combined = lax.dynamic_update_slice(combined, values, (at * share, source, 0, 0))
     combined = combined.reshape(groups * n * width, columns)
 
-    total = None
-    for key in [(0, 0), (0, 1)] + [(j, flip) for j in range(1, pairs) for flip in (0, 1)]:
-        theirs = cot_blocks[key]
-        if key != (0, 0):
-            theirs = after(theirs, lines[ring_order[2] if key[0] else 1][0])
-        term = lax.dot_general(theirs, row_blocks[key], (((1,), (1,)), ((), ())), preferred_element_type=jnp.float32)
-        total = term if total is None else total + term
+    for key in [(j, flip) for j in range(1, pairs) for flip in (0, 1)]:
+        total = total + input_term(key, lines[ring_order[2]][0])
     return (total.astype(jnp.bfloat16), combined)
 
 

time: 213 us -> 193 us (0.906)
  waiting for transfers between devices: 103 us -> 83.7 us
  starting transfers between devices: 38.7 us -> 43.1 us
  other arithmetic: 12.5 us -> 9.11 us
    ppermute x18, waiting for transfers between devices: 29.7 us -> 12 us  [along_tensor(): return lax.ppermute(value, 'tensor', ring)]
    ppermute x9 -> x10, starting transfers between devices: 12.5 us -> 21.6 us  [along_z(): return lax.ppermute(value, 'dp', ring)]
    ppermute x9, waiting for transfers between devices: 28.1 us -> 31.6 us  [along_y(): return lax.ppermute(value, 'dp', ring)]
    ppermute x9 -> x10, waiting for transfers between devices: 39.7 us -> 37 us  [along_z(): return lax.ppermute(value, 'dp', ring)]
    mul x8 -> x9, other arithmetic: 10.2 us -> 7.61 us  [exchanges(): block.reshape(share, 1, width, columns).astype(jnp.float32) * scale[0, 0]]
    ppermute x18, starting transfers between devices: 11.4 us -> 8.85 us  [along_tensor(): return lax.ppermute(value, 'tensor', ring)]
    all_to_all x1, waiting for transfers between devices: 5.22 us -> 3.03 us  [exchanges(): lax.all_to_all(gram, ('dp', 'tensor'), 0, 0, tiled=True)]
    unnamed x45 -> x38, local copies, waits for them, and re-layouts: 6.56 us -> 4.37 us
  transfers between devices with their start and end apart: 37 -> 38, of which waited for: 13 -> 13; matrix products, arithmetic and copies ran while one was open for 15% -> 15% of each run, Pallas kernels for 11% -> 15%
where the time goes in v2:
time: 193 us
  waiting for transfers between devices  83.7 us (43%)
  starting transfers between devices  43.1 us (22%)
  Pallas kernels  30.1 us (16%)
  local copies, waits for them, and re-layouts  17.6 us (9%)
  other arithmetic  9.11 us (5%)
  matrix products  8.06 us (4%)
    ppermute x10, waiting for transfers between devices, along_z(): return lax.ppermute(value, 'dp', ring)  37 us
    ppermute x9, waiting for transfers between devices, along_y(): return lax.ppermute(value, 'dp', ring)  31.6 us
    pallas_call x4, Pallas kernels, exchanges(): pl.pallas_call(functools.partial(grads_kernel, inner, groups, at * inner)...  22.2 us
    ppermute x10, starting transfers between devices, along_z(): return lax.ppermute(value, 'dp', ring)  21.6 us
    ppermute x18, waiting for transfers between devices, along_tensor(): return lax.ppermute(value, 'tensor', ring)  12 us
    dynamic_update_slice x9, local copies, waits for them, and re-layouts, exchanges(): lax.dynamic_update_slice(combined, values, (at * share, source, 0, 0))  8.98 us
    ppermute x9, starting transfers between devices, along_y(): return lax.ppermute(value, 'dp', ring)  8.93 us
    ppermute x18, starting transfers between devices, along_tensor(): return lax.ppermute(value, 'tensor', ring)  8.85 us
  transfers between devices with their start and end apart: 38, of which 13 were waited for; matrix products, arithmetic and copies ran while one was open for 15% of the time, Pallas kernels for 15%

profile of v2, /device:TPU:0, one launch (start us, length us, event | category | flops | bytes accessed | tf_op | source)
XLA Modules:
  0.0 192.7 jit_solution(6729958794626625123)
XLA Ops:
  0.7 1.2 copy-done
  2.0 1.1 pack.3
  3.1 3.1 %collective-permute-start = (bf16[4,128,512]{2,1,0:T(8,128)(2,1)S(1)}, bf16[4,128,512]{2,1,0:T(8,128)(2,1)S(1)}, u32[]{:S(2)}, u32[]{:S(2)}) collective-permute-start(bf16[4,128,512]{2,1,0:T(8,128)(2,1)S(1)} %pack.3), channel_id=1, source_target_pairs={{0,4},{4,0},{8,12},{12,8},{16,20},{20,16},{24,28},{28,24},{1,5},{5... | collective-permute-start | bytes 1572872 | tf_op jit(solution)/shard_map/ppermute | solution.py:256
  6.2 2.6 %collective-permute-start.5 = (bf16[512,512]{1,0:T(8,128)(2,1)}, bf16[512,512]{1,0:T(8,128)(2,1)}, u32[]{:S(2)}, u32[]{:S(2)}) collective-permute-start(bf16[512,512]{1,0:T(8,128)(2,1)} %refs_4_.1), channel_id=1, source_target_pairs={{0,16},{4,20},{8,24},{12,28},{16,0},{20,4},{24,8},{28,12},{1,17},{... | collective-permute-start | bytes 1572872 | tf_op jit(solution)/shard_map/ppermute | solution.py:252
  9.2 1.6 collective-permute-start.16
  10.8 1.2 copy-done.1
  12.0 1.1 pack.2
  13.2 5.7 %collective-permute-done = bf16[4,128,512]{2,1,0:T(8,128)(2,1)S(1)} collective-permute-done((bf16[4,128,512]{2,1,0:T(8,128)(2,1)S(1)}, bf16[4,128,512]{2,1,0:T(8,128)(2,1)S(1)}, u32[]{:S(2)}, u32[]{:S(2)}) %collective-permute-start) | collective-permute-done | bytes 524320 | tf_op jit(solution)/shard_map/ppermute | solution.py:256
  19.0 4.2 %collective-permute-start.1 = (bf16[2,128,512]{2,1,0:T(8,128)(2,1)S(1)}, bf16[2,128,512]{2,1,0:T(8,128)(2,1)S(1)}, u32[]{:S(2)}, u32[]{:S(2)}) collective-permute-start(bf16[2,128,512]{2,1,0:T(8,128)(2,1)S(1)} %pad_maximum_fusion), channel_id=1, source_target_pairs={{0,24},{4,28},{8,16},{12,20},{16,8},{20,12},{24,0},{28,4},{1,25},{... | collective-permute-start | bytes 786440 | tf_op jit(solution)/shard_map/ppermute | solution.py:252
  23.2 1.6 collective-permute-start.8
  24.8 9.7 %collective-permute-done.5.refs_4_ = bf16[512,512]{1,0:T(8,128)(2,1)} collective-permute-done((bf16[512,512]{1,0:T(8,128)(2,1)}, bf16[512,512]{1,0:T(8,128)(2,1)}, u32[]{:S(2)}, u32[]{:S(2)}) %collective-permute-start.5) | collective-permute-done | bytes 524320 | tf_op jit(solution)/shard_map/ppermute | solution.py:252
  34.6 2.0 %collective-permute-start.6 = (bf16[512,512]{1,0:T(8,128)(2,1)}, bf16[512,512]{1,0:T(8,128)(2,1)S(1)}, u32[]{:S(2)}, u32[]{:S(2)}) collective-permute-start(bf16[512,512]{1,0:T(8,128)(2,1)} %collective-permute-done.5.refs_4_), channel_id=1, source_target_pairs={{0,8},{4,12},{8,0},{12,4},{16,24},{20,28},{24,16},{28,20},{1,9},{5... | collective-permute-start | bytes 1572872 | tf_op jit(solution)/shard_map/ppermute | solution.py:252
  36.7 2.2 %collective-permute-done.1.refs_0_ = bf16[2,128,512]{2,1,0:T(8,128)(2,1)S(1)} collective-permute-done((bf16[2,128,512]{2,1,0:T(8,128)(2,1)S(1)}, bf16[2,128,512]{2,1,0:T(8,128)(2,1)S(1)}, u32[]{:S(2)}, u32[]{:S(2)}) %collective-permute-start.1) | collective-permute-done | bytes 262176 | tf_op jit(solution)/shard_map/ppermute | solution.py:252
  38.8 6.9 %collective-permute-start.18 = (bf16[2,128,512]{2,1,0:T(8,128)(2,1)S(1)}, bf16[2,128,512]{2,1,0:T(8,128)(2,1)S(1)}, u32[]{:S(2)}, u32[]{:S(2)}) collective-permute-start(bf16[2,128,512]{2,1,0:T(8,128)(2,1)S(1)} %pad_maximum_fusion.3), channel_id=1, source_target_pairs={{0,16},{4,20},{8,24},{12,28},{16,0},{20,4},{24,8},{28,12},{1,17},{... | collective-permute-start | bytes 786440 | tf_op jit(solution)/shard_map/ppermute | solution.py:252
  45.7 1.5 collective-permute-start.2
  47.8 11.4 %collective-permute-done.18.refs_0_ = bf16[2,128,512]{2,1,0:T(8,128)(2,1)S(1)} collective-permute-done((bf16[2,128,512]{2,1,0:T(8,128)(2,1)S(1)}, bf16[2,128,512]{2,1,0:T(8,128)(2,1)S(1)}, u32[]{:S(2)}, u32[]{:S(2)}) %collective-permute-start.18) | collective-permute-done | bytes 262176 | tf_op jit(solution)/shard_map/ppermute | solution.py:252
  60.0 1.2 collective-permute-done.6.refs_4_
  61.1 0.8 collective-permute-start.22
  62.0 1.5 collective-permute-start.19
  63.6 3.5 %dynamic-slice_bitcast_fusion.1 = (bf16[1024,512]{1,0:T(8,128)(2,1)}, bf16[1024,512]{1,0:T(8,128)(2,1)}, bf16[1024,512]{1,0:T(8,128)(2,1)S(1)}) fusion(bf16[4,1024,512]{2,1,0:T(8,128)(2,1)} %bitcast.48, s32[]{:T(128)S(6)} %select_n.111, s32[]{:T(128)S(6)} %select_n.112, s32[]{:T(128)S(6)} %select_n.109), kind=kLoop, calls=%fused_computation.12 | loop fusion | bytes 6291468 | tf_op jit(solution)/shard_map/jit(dynamic_index_in_dim)/squeeze | solution.py:293
  67.5 6.6 %collective-permute-done.17.refs_5_ = bf16[512,512]{1,0:T(8,128)(2,1)} collective-permute-done((bf16[512,512]{1,0:T(8,128)(2,1)S(1)}, bf16[512,512]{1,0:T(8,128)(2,1)}, u32[]{:S(2)}, u32[]{:S(2)}) %collective-permute-start.17) | collective-permute-done | bytes 524320 | tf_op jit(solution)/shard_map/ppermute | solution.py:256
  74.9 10.4 %collective-permute-done.22.refs_5_ = bf16[512,512]{1,0:T(8,128)(2,1)S(1)} collective-permute-done((bf16[512,512]{1,0:T(8,128)(2,1)}, bf16[512,512]{1,0:T(8,128)(2,1)S(1)}, u32[]{:S(2)}, u32[]{:S(2)}) %collective-permute-start.22) | collective-permute-done | bytes 524320 | tf_op jit(solution)/shard_map/ppermute | solution.py:256
  86.2 0.7 copy-done.17
  87.2 0.6 stack.77.index_ref
  87.9 4.7 %shard_map.50 = (f32[2,512,512]{2,1,0:T(8,128)}, f32[1,1,128]{2,1,0:T(1,128)}) custom-call(s32[12]{0:T(128)} %stack.77.index_ref, bf16[2,128,512]{2,1,0:T(8,128)(2,1)} %copy-done.4, bf16[2,128,512]{2,1,0:T(8,128)(2,1)} %collective-permute-done.8.refs_1_, bf16[2,128,512]{2,1,0:T(8,128)(2,1)} %copy-done.11, bf16[2,128,512]{2,1,0:T(8,128)(2,1)} %copy-done.12, ...), custom_call_target="tpu_custom_call" | custom-call | flops 536870912 | bytes 4194304 | tf_op jit(solution)/shard_map/pallas_call | solution.py:330
  92.6 4.8 %shard_map.51 = (f32[2,512,512]{2,1,0:T(8,128)}, f32[1,1,128]{2,1,0:T(1,128)}) custom-call(s32[12]{0:T(128)} %stack.77.index_ref, bf16[2,128,512]{2,1,0:T(8,128)(2,1)} %collective-permute-done.12.refs_0_, bf16[2,128,512]{2,1,0:T(8,128)(2,1)} %collective-permute-done.13.refs_1_, bf16[2,128,512]{2,1,0:T(8,128)(2,1)} %collective-permute-done.14.refs_2_, ...), custom_call_target="tpu_custom_call" | custom-call | flops 536870912 | bytes 4194304 | tf_op jit(solution)/shard_map/pallas_call | solution.py:330
  97.4 5.5 %shard_map.52 = (f32[2,512,512]{2,1,0:T(8,128)}, f32[1,1,128]{2,1,0:T(1,128)}) custom-call(s32[12]{0:T(128)} %stack.77.index_ref, bf16[2,128,512]{2,1,0:T(8,128)(2,1)} %copy-done.14, bf16[2,128,512]{2,1,0:T(8,128)(2,1)} %copy-done.15, bf16[2,128,512]{2,1,0:T(8,128)(2,1)} %copy-done.16, bf16[2,128,512]{2,1,0:T(8,128)(2,1)} %copy-done.17, ...), custom_call_target="tpu_custom_call" | custom-call | flops 536870912 | bytes 4194304 | tf_op jit(solution)/shard_map/pallas_call | solution.py:330
  103.0 1.6 collective-permute-start.25
  104.6 7.2 %shard_map.53 = (f32[2,512,512]{2,1,0:T(8,128)}, f32[32,1,128]{2,1,0:T(1,128)}) custom-call(s32[12]{0:T(128)} %stack.77.index_ref, bf16[2,128,512]{2,1,0:T(8,128)(2,1)} %copy-done.9, bf16[2,128,512]{2,1,0:T(8,128)(2,1)} %copy-done.10, bf16[2,128,512]{2,1,0:T(8,128)(2,1)} %collective-permute-done.3.refs_2_, ...), custom_call_target="tpu_custom_call" | custom-call | flops 536870912 | bytes 4194304 | tf_op jit(solution)/shard_map/pallas_call | solution.py:330
  111.7 3.8 %all-to-all-start = ((f32[32,1,128]{2,1,0:T(1,128)}), f32[32,1,128]{2,1,0:T(1,128)S(1)}, u32[]{:S(2)}, u32[]{:S(2)}) async-start(f32[32,1,128]{2,1,0:T(1,128)} %get-tuple-element.23), calls=%async_computation | async-start | bytes 32768 | tf_op jit(solution)/shard_map/all_to_all | solution.py:352
  115.5 2.0 %fusion = f32[512,1024]{1,0:T(8,128)S(1)} fusion(bf16[512,512]{1,0:T(8,128)(2,1)S(1)} %copy-done.3, bf16[4,1024,512]{2,1,0:T(8,128)(2,1)} %bitcast.49, s32[]{:T(128)S(6)} %select_n.108), kind=kOutput, calls=%fused_computation.2 | convolution fusion | flops 536870912 | bytes 3670020 | tf_op jit(solution)/shard_map/dot_general | solution.py:355
  117.5 2.1 %convolution_add_fusion = f32[512,1024]{1,0:T(8,128)S(1)} fusion(f32[512,1024]{1,0:T(8,128)S(1)} %fusion, bf16[512,512]{1,0:T(8,128)(2,1)} %collective-permute-done.23, bf16[1024,512]{1,0:T(8,128)(2,1)} %collective-permute-done.24), kind=kOutput, calls=%fused_computation.1 | convolution fusion | flops 537395200 | bytes 5767168 | tf_op jit(solution)/shard_map/dot_general | solution.py:355
  119.6 3.0 %all-to-all-done.gram_ref = f32[32,1,128]{2,1,0:T(1,128)S(1)} async-done(((f32[32,1,128]{2,1,0:T(1,128)}), f32[32,1,128]{2,1,0:T(1,128)S(1)}, u32[]{:S(2)}, u32[]{:S(2)}) %all-to-all-start) | async-done | bytes 16416 | tf_op jit(solution)/shard_map/all_to_all | solution.py:352
  123.3 5.6 %combine.1 = (f32[512,512]{1,0:T(8,128)}, f32[1,1]{1,0:T(1,128)}) custom-call(s32[12]{0:T(128)} %stack.77.index_ref, f32[32,1,128]{2,1,0:T(1,128)} %copy-done.18, f32[2,512,512]{2,1,0:T(8,128)} %get-tuple-element.17.refs_6_.refs_0_, f32[2,512,512]{2,1,0:T(8,128)} %get-tuple-element.19.refs_7_.refs_1_, f32[2,512,512]{2,1,0:T(8,128)} %get-tuple-element.21.refs_8_.refs_2_, ...), custom_call_target="tpu_custom_call" | custom-call | flops 4194304 | bytes 8388608 | tf_op jit(solution)/shard_map/combine/pallas_call | solution.py:364
  128.9 1.3 convert_element_type.114
  130.8 0.6 collective-permute-start.27
  131.5 2.4 %collective-permute-start.26 = (f16[512,512]{1,0:T(8,128)(2,1)S(1)}, f16[512,512]{1,0:T(8,128)(2,1)S(1)}, u32[]{:S(2)}, u32[]{:S(2)}) collective-permute-start(f16[512,512]{1,0:T(8,128)(2,1)S(1)} %convert_element_type.114), channel_id=1, source_target_pairs={{0,24},{4,28},{8,0},{12,4},{16,8},{20,12},{24,16},{28,20},{1,25},{... | collective-permute-start | bytes 1572872 | tf_op jit(solution)/shard_map/ppermute | solution.py:252
  133.9 0.7 convert_multiply_fusion.6
  134.6 1.0 constant_dynamic-update-slice_fusion.8
  135.7 8.4 %collective-permute-done.30 = f16[512,512]{1,0:T(8,128)(2,1)} collective-permute-done((f16[512,512]{1,0:T(8,128)(2,1)S(1)}, f16[512,512]{1,0:T(8,128)(2,1)}, u32[]{:S(2)}, u32[]{:S(2)}) %collective-permute-start.30) | collective-permute-done | bytes 524320 | tf_op jit(solution)/shard_map/ppermute | solution.py:256
  144.1 1.8 convert_multiply_fusion.5
  145.9 1.0 constant_dynamic-update-slice_fusion.7
  146.9 0.7 collective-permute-start.33
  147.6 10.3 %collective-permute-done.31 = f16[512,512]{1,0:T(8,128)(2,1)S(1)} collective-permute-done((f16[512,512]{1,0:T(8,128)(2,1)S(1)}, f16[512,512]{1,0:T(8,128)(2,1)S(1)}, u32[]{:S(2)}, u32[]{:S(2)}) %collective-permute-start.31) | collective-permute-done | bytes 524320 | tf_op jit(solution)/shard_map/ppermute | solution.py:252
  158.5 1.6 collective-permute-start.34
  160.0 0.7 convert_multiply_fusion.4
  160.8 0.8 convert_multiply_fusion.2
  161.5 2.1 %fusion.6 = f32[512,1024]{1,0:T(8,128)S(1)} fusion(bf16[512,512]{1,0:T(8,128)(2,1)} %collective-permute-done.25, bf16[1024,512]{1,0:T(8,128)(2,1)} %collective-permute-done.27), kind=kOutput, calls=%fused_computation.35 | convolution fusion | flops 536870912 | bytes 3670016 | tf_op jit(solution)/shard_map/dot_general | solution.py:355
  163.7 1.0 constant_dynamic-update-slice_fusion.6
  164.7 12.0 %collective-permute-done.29 = bf16[1024,512]{1,0:T(8,128)(2,1)S(1)} collective-permute-done((bf16[1024,512]{1,0:T(8,128)(2,1)}, bf16[1024,512]{1,0:T(8,128)(2,1)S(1)}, u32[]{:S(2)}, u32[]{:S(2)}) %collective-permute-start.29) | collective-permute-done | bytes 1048608 | tf_op jit(solution)/shard_map/ppermute | solution.py:260
  176.7 1.8 add_convert_fusion
  178.6 1.6 collective-permute-start.35
  180.6 0.7 convert_multiply_fusion.3
  181.4 1.0 constant_dynamic-update-slice_fusion.5
  182.4 1.0 constant_dynamic-update-slice_fusion.4
  183.4 0.7 convert_multiply_fusion
  184.2 0.7 convert_multiply_fusion.1
  185.0 1.0 constant_dynamic-update-slice_fusion.3
  186.0 1.0 constant_dynamic-update-slice_fusion.2
  187.5 0.7 convert_multiply_fusion.8
  188.2 0.8 constant_dynamic-update-slice_fusion.1
  189.0 2.2 %collective-permute-done.36 = f16[256,512]{1,0:T(8,128)(2,1)S(1)} collective-permute-done((f16[256,512]{1,0:T(8,128)(2,1)S(1)}, f16[256,512]{1,0:T(8,128)(2,1)S(1)}, u32[]{:S(2)}, u32[]{:S(2)}) %collective-permute-start.36) | collective-permute-done | bytes 262176 | tf_op jit(solution)/shard_map/ppermute | solution.py:252
  191.2 0.7 convert_multiply_fusion.7
  191.9 0.8 constant_dynamic-update-slice_fusion
  (92 shorter events, 7.4 us)
Async XLA Ops:
  0.7 1.2 copy-start
  2.0 84.9 %copy-start.2 = (bf16[512,512]{1,0:T(8,128)(2,1)S(1)}, bf16[512,512]{1,0:T(8,128)(2,1)}, u32[]{:S(2)}) copy-start(bf16[512,512]{1,0:T(8,128)(2,1)} %refs_4_.1) | copy-start | bytes 1572868
  3.1 15.8 %collective-permute-start = (bf16[4,128,512]{2,1,0:T(8,128)(2,1)S(1)}, bf16[4,128,512]{2,1,0:T(8,128)(2,1)S(1)}, u32[]{:S(2)}, u32[]{:S(2)}) collective-permute-start(bf16[4,128,512]{2,1,0:T(8,128)(2,1)S(1)} %pack.3), channel_id=1, source_target_pairs={{0,4},{4,0},{8,12},{12,8},{16,20},{20,16},{24,28},{28,24},{1,5},{5... | collective-permute-start | bytes 1572872 | tf_op jit(solution)/shard_map/ppermute | solution.py:256
  6.2 28.4 %collective-permute-start.5 = (bf16[512,512]{1,0:T(8,128)(2,1)}, bf16[512,512]{1,0:T(8,128)(2,1)}, u32[]{:S(2)}, u32[]{:S(2)}) collective-permute-start(bf16[512,512]{1,0:T(8,128)(2,1)} %refs_4_.1), channel_id=1, source_target_pairs={{0,16},{4,20},{8,24},{12,28},{16,0},{20,4},{24,8},{28,12},{1,17},{... | collective-permute-start | bytes 1572872 | tf_op jit(solution)/shard_map/ppermute | solution.py:252
  8.7 25.8 %collective-permute-start.11 = (bf16[512,512]{1,0:T(8,128)(2,1)}, bf16[512,512]{1,0:T(8,128)(2,1)S(1)}, u32[]{:S(2)}, u32[]{:S(2)}) collective-permute-start(bf16[512,512]{1,0:T(8,128)(2,1)} %refs_4_.1), channel_id=1, source_target_pairs={{0,4},{4,0},{8,12},{12,8},{16,20},{20,16},{24,28},{28,24},{1,5},{5... | collective-permute-start | bytes 1572872 | tf_op jit(solution)/shard_map/ppermute | solution.py:256
  9.2 25.4 %collective-permute-start.16 = (bf16[512,512]{1,0:T(8,128)(2,1)}, bf16[512,512]{1,0:T(8,128)(2,1)S(1)}, u32[]{:S(2)}, u32[]{:S(2)}) collective-permute-start(bf16[512,512]{1,0:T(8,128)(2,1)} %refs_4_.1), channel_id=1, source_target_pairs={{0,8},{4,12},{8,0},{12,4},{16,24},{20,28},{24,16},{28,20},{1,9},{5... | collective-permute-start | bytes 1572872 | tf_op jit(solution)/shard_map/ppermute | solution.py:252
  10.8 1.2 copy-start.1
  19.0 19.8 %collective-permute-start.1 = (bf16[2,128,512]{2,1,0:T(8,128)(2,1)S(1)}, bf16[2,128,512]{2,1,0:T(8,128)(2,1)S(1)}, u32[]{:S(2)}, u32[]{:S(2)}) collective-permute-start(bf16[2,128,512]{2,1,0:T(8,128)(2,1)S(1)} %pad_maximum_fusion), channel_id=1, source_target_pairs={{0,24},{4,28},{8,16},{12,20},{16,8},{20,12},{24,0},{28,4},{1,25},{... | collective-permute-start | bytes 786440 | tf_op jit(solution)/shard_map/ppermute | solution.py:252
  23.2 64.7 %copy-start.4 = (bf16[2,128,512]{2,1,0:T(8,128)(2,1)}, bf16[2,128,512]{2,1,0:T(8,128)(2,1)S(1)}, u32[]{:S(2)}) copy-start(bf16[2,128,512]{2,1,0:T(8,128)(2,1)S(1)} %pad_maximum_fusion.1.refs_0_) | copy-start | bytes 786436
  23.2 22.5 %collective-permute-start.8 = (bf16[2,128,512]{2,1,0:T(8,128)(2,1)S(1)}, bf16[2,128,512]{2,1,0:T(8,128)(2,1)}, u32[]{:S(2)}, u32[]{:S(2)}) collective-permute-start(bf16[2,128,512]{2,1,0:T(8,128)(2,1)S(1)} %pad_maximum_fusion.1.refs_0_), channel_id=1, source_target_pairs={{0,2},{1,3},{2,0},{3,1},{4,6},{5,7},{6,4},{7,5},{8,10},{9,11},{10,... | collective-permute-start | bytes 786440 | tf_op jit(solution)/shard_map/ppermute | solution.py:260
  34.5 12.7 %collective-permute-start.9 = (bf16[2,128,512]{2,1,0:T(8,128)(2,1)S(1)}, bf16[2,128,512]{2,1,0:T(8,128)(2,1)S(1)}, u32[]{:S(2)}, u32[]{:S(2)}) collective-permute-start(bf16[2,128,512]{2,1,0:T(8,128)(2,1)S(1)} %pad_maximum_fusion.1.refs_0_), channel_id=1, source_target_pairs={{0,1},{1,0},{2,3},{3,2},{4,5},{5,4},{6,7},{7,6},{8,9},{9,8},{10,11... | collective-permute-start | bytes 786440 | tf_op jit(solution)/shard_map/ppermute | solution.py:260
  34.5 53.3 %copy-start.6 = (bf16[512,512]{1,0:T(8,128)(2,1)}, bf16[512,512]{1,0:T(8,128)(2,1)S(1)}, u32[]{:S(2)}) copy-start(bf16[512,512]{1,0:T(8,128)(2,1)S(1)} %collective-permute-done.11.refs_5_) | copy-start | bytes 1572868
  34.5 12.7 %collective-permute-start.12 = (bf16[2,128,512]{2,1,0:T(8,128)(2,1)S(1)}, bf16[2,128,512]{2,1,0:T(8,128)(2,1)}, u32[]{:S(2)}, u32[]{:S(2)}) collective-permute-start(bf16[2,128,512]{2,1,0:T(8,128)(2,1)S(1)} %pad_maximum_fusion.2), channel_id=1, source_target_pairs={{0,8},{4,12},{8,0},{12,4},{16,24},{20,28},{24,16},{28,20},{1,9},{5... | collective-permute-start | bytes 786440 | tf_op jit(solution)/shard_map/ppermute | solution.py:252
  34.6 58.0 %copy-start.5 = (bf16[512,512]{1,0:T(8,128)(2,1)}, bf16[512,512]{1,0:T(8,128)(2,1)S(1)}, u32[]{:S(2)}) copy-start(bf16[512,512]{1,0:T(8,128)(2,1)S(1)} %collective-permute-done.16.refs_4_) | copy-start | bytes 1572868
  34.6 26.5 %collective-permute-start.6 = (bf16[512,512]{1,0:T(8,128)(2,1)}, bf16[512,512]{1,0:T(8,128)(2,1)S(1)}, u32[]{:S(2)}, u32[]{:S(2)}) collective-permute-start(bf16[512,512]{1,0:T(8,128)(2,1)} %collective-permute-done.5.refs_4_), channel_id=1, source_target_pairs={{0,8},{4,12},{8,0},{12,4},{16,24},{20,28},{24,16},{28,20},{1,9},{5... | collective-permute-start | bytes 1572872 | tf_op jit(solution)/shard_map/ppermute | solution.py:252
  38.8 24.7 %copy-start.9 = (bf16[2,128,512]{2,1,0:T(8,128)(2,1)}, bf16[2,128,512]{2,1,0:T(8,128)(2,1)S(1)}, u32[]{:S(2)}) copy-start(bf16[2,128,512]{2,1,0:T(8,128)(2,1)S(1)} %collective-permute-done.1.refs_0_) | copy-start | bytes 786436
  38.8 20.4 %collective-permute-start.18 = (bf16[2,128,512]{2,1,0:T(8,128)(2,1)S(1)}, bf16[2,128,512]{2,1,0:T(8,128)(2,1)S(1)}, u32[]{:S(2)}, u32[]{:S(2)}) collective-permute-start(bf16[2,128,512]{2,1,0:T(8,128)(2,1)S(1)} %pad_maximum_fusion.3), channel_id=1, source_target_pairs={{0,16},{4,20},{8,24},{12,28},{16,0},{20,4},{24,8},{28,12},{1,17},{... | collective-permute-start | bytes 786440 | tf_op jit(solution)/shard_map/ppermute | solution.py:252
  45.7 14.1 %collective-permute-start.2 = (bf16[2,128,512]{2,1,0:T(8,128)(2,1)S(1)}, bf16[2,128,512]{2,1,0:T(8,128)(2,1)S(1)}, u32[]{:S(2)}, u32[]{:S(2)}) collective-permute-start(bf16[2,128,512]{2,1,0:T(8,128)(2,1)S(1)} %collective-permute-done.1.refs_0_), channel_id=1, source_target_pairs={{0,2},{1,3},{2,0},{3,1},{4,6},{5,7},{6,4},{7,5},{8,10},{9,11},{10,... | collective-permute-start | bytes 786440 | tf_op jit(solution)/shard_map/ppermute | solution.py:260
  47.2 16.3 %copy-start.11 = (bf16[2,128,512]{2,1,0:T(8,128)(2,1)}, bf16[2,128,512]{2,1,0:T(8,128)(2,1)S(1)}, u32[]{:S(2)}) copy-start(bf16[2,128,512]{2,1,0:T(8,128)(2,1)S(1)} %collective-permute-done.9.refs_2_) | copy-start | bytes 786436
  47.2 14.8 %collective-permute-start.10 = (bf16[2,128,512]{2,1,0:T(8,128)(2,1)}, bf16[2,128,512]{2,1,0:T(8,128)(2,1)S(1)}, u32[]{:S(2)}, u32[]{:S(2)}) collective-permute-start(bf16[2,128,512]{2,1,0:T(8,128)(2,1)} %collective-permute-done.8.refs_1_), channel_id=1, source_target_pairs={{0,1},{1,0},{2,3},{3,2},{4,5},{5,4},{6,7},{7,6},{8,9},{9,8},{10,11... | collective-permute-start | bytes 786440 | tf_op jit(solution)/shard_map/ppermute | solution.py:260
  47.2 16.3 %collective-permute-start.13 = (bf16[2,128,512]{2,1,0:T(8,128)(2,1)}, bf16[2,128,512]{2,1,0:T(8,128)(2,1)}, u32[]{:S(2)}, u32[]{:S(2)}) collective-permute-start(bf16[2,128,512]{2,1,0:T(8,128)(2,1)} %collective-permute-done.12.refs_0_), channel_id=1, source_target_pairs={{0,2},{1,3},{2,0},{3,1},{4,6},{5,7},{6,4},{7,5},{8,10},{9,11},{10,... | collective-permute-start | bytes 786440 | tf_op jit(solution)/shard_map/ppermute | solution.py:260
  59.3 0.7 copy-start.14
  59.3 14.9 %collective-permute-start.17 = (bf16[512,512]{1,0:T(8,128)(2,1)S(1)}, bf16[512,512]{1,0:T(8,128)(2,1)}, u32[]{:S(2)}, u32[]{:S(2)}) collective-permute-start(bf16[512,512]{1,0:T(8,128)(2,1)S(1)} %collective-permute-done.16.refs_4_), channel_id=1, source_target_pairs={{0,4},{4,0},{8,12},{12,8},{16,20},{20,16},{24,28},{28,24},{1,5},{5... | collective-permute-start | bytes 1572872 | tf_op jit(solution)/shard_map/ppermute | solution.py:256
  60.0 3.6 %copy-start.10 = (bf16[2,128,512]{2,1,0:T(8,128)(2,1)}, bf16[2,128,512]{2,1,0:T(8,128)(2,1)S(1)}, u32[]{:S(2)}) copy-start(bf16[2,128,512]{2,1,0:T(8,128)(2,1)S(1)} %collective-permute-done.2.refs_1_) | copy-start | bytes 786436
  60.0 7.1 %collective-permute-start.14 = (bf16[2,128,512]{2,1,0:T(8,128)(2,1)}, bf16[2,128,512]{2,1,0:T(8,128)(2,1)}, u32[]{:S(2)}, u32[]{:S(2)}) collective-permute-start(bf16[2,128,512]{2,1,0:T(8,128)(2,1)} %collective-permute-done.12.refs_0_), channel_id=1, source_target_pairs={{0,1},{1,0},{2,3},{3,2},{4,5},{5,4},{6,7},{7,6},{8,9},{9,8},{10,11... | collective-permute-start | bytes 786440 | tf_op jit(solution)/shard_map/ppermute | solution.py:260
  61.1 2.4 %copy-start.7 = (bf16[512,512]{1,0:T(8,128)(2,1)}, bf16[512,512]{1,0:T(8,128)(2,1)S(1)}, u32[]{:S(2)}) copy-start(bf16[512,512]{1,0:T(8,128)(2,1)S(1)} %collective-permute-done.6.refs_4_) | copy-start | bytes 1572868
  61.1 24.2 %collective-permute-start.22 = (bf16[512,512]{1,0:T(8,128)(2,1)}, bf16[512,512]{1,0:T(8,128)(2,1)S(1)}, u32[]{:S(2)}, u32[]{:S(2)}) collective-permute-start(bf16[512,512]{1,0:T(8,128)(2,1)} %collective-permute-done.5.refs_4_), channel_id=1, source_target_pairs={{0,4},{4,0},{8,12},{12,8},{16,20},{20,16},{24,28},{28,24},{1,5},{5... | collective-permute-start | bytes 1572872 | tf_op jit(solution)/shard_map/ppermute | solution.py:256
  62.0 1.6 copy-start.12
  62.0 12.2 %collective-permute-start.19 = (bf16[2,128,512]{2,1,0:T(8,128)(2,1)}, bf16[2,128,512]{2,1,0:T(8,128)(2,1)S(1)}, u32[]{:S(2)}, u32[]{:S(2)}) collective-permute-start(bf16[2,128,512]{2,1,0:T(8,128)(2,1)} %copy-done.14), channel_id=1, source_target_pairs={{0,2},{1,3},{2,0},{3,1},{4,6},{5,7},{6,4},{7,5},{8,10},{9,11},{10,... | collective-permute-start | bytes 786440 | tf_op jit(solution)/shard_map/ppermute | solution.py:260
  63.5 11.2 %collective-permute-start.20 = (bf16[2,128,512]{2,1,0:T(8,128)(2,1)}, bf16[2,128,512]{2,1,0:T(8,128)(2,1)S(1)}, u32[]{:S(2)}, u32[]{:S(2)}) collective-permute-start(bf16[2,128,512]{2,1,0:T(8,128)(2,1)} %copy-done.14), channel_id=1, source_target_pairs={{0,1},{1,0},{2,3},{3,2},{4,5},{5,4},{6,7},{7,6},{8,9},{9,8},{10,11... | collective-permute-start | bytes 786440 | tf_op jit(solution)/shard_map/ppermute | solution.py:260
  63.6 39.4 %copy-start.3 = (bf16[512,512]{1,0:T(8,128)(2,1)S(1)}, bf16[512,512]{1,0:T(8,128)(2,1)}, u32[]{:S(2)}) copy-start(bf16[512,512]{1,0:T(8,128)(2,1)} %refs_4_.1) | copy-start | bytes 1572868
  67.0 50.4 %collective-permute-start.24 = (bf16[1024,512]{1,0:T(8,128)(2,1)S(1)}, bf16[1024,512]{1,0:T(8,128)(2,1)}, u32[]{:S(2)}, u32[]{:S(2)}) collective-permute-start(bf16[1024,512]{1,0:T(8,128)(2,1)S(1)} %get-tuple-element.34), channel_id=1, source_target_pairs={{0,1},{1,0},{2,3},{3,2},{4,5},{5,4},{6,7},{7,6},{8,9},{9,8},{10,11... | collective-permute-start | bytes 3145736 | tf_op jit(solution)/shard_map/ppermute | solution.py:260
  74.2 11.1 %collective-permute-start.15 = (bf16[2,128,512]{2,1,0:T(8,128)(2,1)}, bf16[2,128,512]{2,1,0:T(8,128)(2,1)S(1)}, u32[]{:S(2)}, u32[]{:S(2)}) collective-permute-start(bf16[2,128,512]{2,1,0:T(8,128)(2,1)} %collective-permute-done.13.refs_1_), channel_id=1, source_target_pairs={{0,1},{1,0},{2,3},{3,2},{4,5},{5,4},{6,7},{7,6},{8,9},{9,8},{10,11... | collective-permute-start | bytes 786440 | tf_op jit(solution)/shard_map/ppermute | solution.py:260
  74.2 11.9 %copy-start.15 = (bf16[2,128,512]{2,1,0:T(8,128)(2,1)}, bf16[2,128,512]{2,1,0:T(8,128)(2,1)S(1)}, u32[]{:S(2)}) copy-start(bf16[2,128,512]{2,1,0:T(8,128)(2,1)S(1)} %collective-permute-done.19.refs_1_) | copy-start | bytes 786436
  74.2 30.4 %collective-permute-start.7 = (bf16[512,512]{1,0:T(8,128)(2,1)}, bf16[512,512]{1,0:T(8,128)(2,1)}, u32[]{:S(2)}, u32[]{:S(2)}) collective-permute-start(bf16[512,512]{1,0:T(8,128)(2,1)} %copy-done.7), channel_id=1, source_target_pairs={{0,4},{4,0},{8,12},{12,8},{16,20},{20,16},{24,28},{28,24},{1,5},{5... | collective-permute-start | bytes 1572872 | tf_op jit(solution)/shard_map/ppermute | solution.py:256
  74.8 11.4 %copy-start.16 = (bf16[2,128,512]{2,1,0:T(8,128)(2,1)}, bf16[2,128,512]{2,1,0:T(8,128)(2,1)S(1)}, u32[]{:S(2)}) copy-start(bf16[2,128,512]{2,1,0:T(8,128)(2,1)S(1)} %collective-permute-done.20.refs_2_) | copy-start | bytes 786436
  74.8 11.3 %collective-permute-start.21 = (bf16[2,128,512]{2,1,0:T(8,128)(2,1)S(1)}, bf16[2,128,512]{2,1,0:T(8,128)(2,1)S(1)}, u32[]{:S(2)}, u32[]{:S(2)}) collective-permute-start(bf16[2,128,512]{2,1,0:T(8,128)(2,1)S(1)} %collective-permute-done.19.refs_1_), channel_id=1, source_target_pairs={{0,1},{1,0},{2,3},{3,2},{4,5},{5,4},{6,7},{7,6},{8,9},{9,8},{10,11... | collective-permute-start | bytes 786440 | tf_op jit(solution)/shard_map/ppermute | solution.py:260
  85.3 0.8 copy-start.8
  85.3 17.7 %collective-permute-start.3 = (bf16[2,128,512]{2,1,0:T(8,128)(2,1)}, bf16[2,128,512]{2,1,0:T(8,128)(2,1)}, u32[]{:S(2)}, u32[]{:S(2)}) collective-permute-start(bf16[2,128,512]{2,1,0:T(8,128)(2,1)} %copy-done.9), channel_id=1, source_target_pairs={{0,1},{1,0},{2,3},{3,2},{4,5},{5,4},{6,7},{7,6},{8,9},{9,8},{10,11... | collective-permute-start | bytes 786440 | tf_op jit(solution)/shard_map/ppermute | solution.py:260
  85.3 0.9 copy-start.13
  85.3 19.2 %collective-permute-start.4 = (bf16[2,128,512]{2,1,0:T(8,128)(2,1)}, bf16[2,128,512]{2,1,0:T(8,128)(2,1)}, u32[]{:S(2)}, u32[]{:S(2)}) collective-permute-start(bf16[2,128,512]{2,1,0:T(8,128)(2,1)} %copy-done.10), channel_id=1, source_target_pairs={{0,1},{1,0},{2,3},{3,2},{4,5},{5,4},{6,7},{7,6},{8,9},{9,8},{10,11... | collective-permute-start | bytes 786440 | tf_op jit(solution)/shard_map/ppermute | solution.py:260
  86.2 0.7 copy-start.17
  86.9 30.5 %collective-permute-start.23 = (bf16[512,512]{1,0:T(8,128)(2,1)S(1)}, bf16[512,512]{1,0:T(8,128)(2,1)}, u32[]{:S(2)}, u32[]{:S(2)}) collective-permute-start(bf16[512,512]{1,0:T(8,128)(2,1)S(1)} %copy-done.2), channel_id=1, source_target_pairs={{0,1},{1,0},{2,3},{3,2},{4,5},{5,4},{6,7},{7,6},{8,9},{9,8},{10,11... | collective-permute-start | bytes 1572872 | tf_op jit(solution)/shard_map/ppermute | solution.py:260
  103.0 28.5 %collective-permute-start.25 = (bf16[512,512]{1,0:T(8,128)(2,1)S(1)}, bf16[512,512]{1,0:T(8,128)(2,1)}, u32[]{:S(2)}, u32[]{:S(2)}) collective-permute-start(bf16[512,512]{1,0:T(8,128)(2,1)S(1)} %copy-done.3), channel_id=1, source_target_pairs={{0,2},{1,3},{2,0},{3,1},{4,6},{5,7},{6,4},{7,5},{8,10},{9,11},{10,... | collective-permute-start | bytes 1572872 | tf_op jit(solution)/shard_map/ppermute | solution.py:260
  111.7 10.9 %all-to-all-start = ((f32[32,1,128]{2,1,0:T(1,128)}), f32[32,1,128]{2,1,0:T(1,128)S(1)}, u32[]{:S(2)}, u32[]{:S(2)}) async-start(f32[32,1,128]{2,1,0:T(1,128)} %get-tuple-element.23), calls=%async_computation | async-start | bytes 32768 | tf_op jit(solution)/shard_map/all_to_all | solution.py:352
  122.7 0.6 copy-start.18
  130.2 13.9 %collective-permute-start.30 = (f16[512,512]{1,0:T(8,128)(2,1)S(1)}, f16[512,512]{1,0:T(8,128)(2,1)}, u32[]{:S(2)}, u32[]{:S(2)}) collective-permute-start(f16[512,512]{1,0:T(8,128)(2,1)S(1)} %convert_element_type.114), channel_id=1, source_target_pairs={{0,4},{4,0},{8,12},{12,8},{16,20},{20,16},{24,28},{28,24},{1,5},{5... | collective-permute-start | bytes 1572872 | tf_op jit(solution)/shard_map/ppermute | solution.py:256
  130.8 30.7 %collective-permute-start.27 = (bf16[1024,512]{1,0:T(8,128)(2,1)}, bf16[1024,512]{1,0:T(8,128)(2,1)}, u32[]{:S(2)}, u32[]{:S(2)}) collective-permute-start(bf16[1024,512]{1,0:T(8,128)(2,1)} %get-tuple-element.32), channel_id=1, source_target_pairs={{0,2},{1,3},{2,0},{3,1},{4,6},{5,7},{6,4},{7,5},{8,10},{9,11},{10,... | collective-permute-start | bytes 3145736 | tf_op jit(solution)/shard_map/ppermute | solution.py:260
  131.5 15.5 %collective-permute-start.28 = (bf16[512,512]{1,0:T(8,128)(2,1)}, bf16[512,512]{1,0:T(8,128)(2,1)S(1)}, u32[]{:S(2)}, u32[]{:S(2)}) collective-permute-start(bf16[512,512]{1,0:T(8,128)(2,1)} %collective-permute-done.25), channel_id=1, source_target_pairs={{0,1},{1,0},{2,3},{3,2},{4,5},{5,4},{6,7},{7,6},{8,9},{9,8},{10,11... | collective-permute-start | bytes 1572872 | tf_op jit(solution)/shard_map/ppermute | solution.py:260
  131.5 15.5 %collective-permute-start.26 = (f16[512,512]{1,0:T(8,128)(2,1)S(1)}, f16[512,512]{1,0:T(8,128)(2,1)S(1)}, u32[]{:S(2)}, u32[]{:S(2)}) collective-permute-start(f16[512,512]{1,0:T(8,128)(2,1)S(1)} %convert_element_type.114), channel_id=1, source_target_pairs={{0,24},{4,28},{8,0},{12,4},{16,8},{20,12},{24,16},{28,20},{1,25},{... | collective-permute-start | bytes 1572872 | tf_op jit(solution)/shard_map/ppermute | solution.py:252
  133.9 24.0 %collective-permute-start.31 = (f16[512,512]{1,0:T(8,128)(2,1)S(1)}, f16[512,512]{1,0:T(8,128)(2,1)S(1)}, u32[]{:S(2)}, u32[]{:S(2)}) collective-permute-start(f16[512,512]{1,0:T(8,128)(2,1)S(1)} %convert_element_type.114), channel_id=1, source_target_pairs={{0,8},{4,12},{8,16},{12,20},{16,24},{20,28},{24,0},{28,4},{1,9},{5... | collective-permute-start | bytes 1572872 | tf_op jit(solution)/shard_map/ppermute | solution.py:252
  144.1 32.6 %collective-permute-start.29 = (bf16[1024,512]{1,0:T(8,128)(2,1)}, bf16[1024,512]{1,0:T(8,128)(2,1)S(1)}, u32[]{:S(2)}, u32[]{:S(2)}) collective-permute-start(bf16[1024,512]{1,0:T(8,128)(2,1)} %get-tuple-element.33), channel_id=1, source_target_pairs={{0,3},{1,2},{2,1},{3,0},{4,7},{5,6},{6,5},{7,4},{8,11},{9,10},{10,... | collective-permute-start | bytes 3145736 | tf_op jit(solution)/shard_map/ppermute | solution.py:260
  146.9 37.3 %collective-permute-start.33 = (f16[512,512]{1,0:T(8,128)(2,1)S(1)}, f16[512,512]{1,0:T(8,128)(2,1)S(1)}, u32[]{:S(2)}, u32[]{:S(2)}) collective-permute-start(f16[512,512]{1,0:T(8,128)(2,1)S(1)} %collective-permute-done.26), channel_id=1, source_target_pairs={{0,4},{4,0},{8,12},{12,8},{16,20},{20,16},{24,28},{28,24},{1,5},{5... | collective-permute-start | bytes 1572872 | tf_op jit(solution)/shard_map/ppermute | solution.py:256
  157.9 22.3 %collective-permute-start.32 = (f16[512,512]{1,0:T(8,128)(2,1)S(1)}, f16[512,512]{1,0:T(8,128)(2,1)S(1)}, u32[]{:S(2)}, u32[]{:S(2)}) collective-permute-start(f16[512,512]{1,0:T(8,128)(2,1)S(1)} %collective-permute-done.31), channel_id=1, source_target_pairs={{0,4},{4,0},{8,12},{12,8},{16,20},{20,16},{24,28},{28,24},{1,5},{5... | collective-permute-start | bytes 1572872 | tf_op jit(solution)/shard_map/ppermute | solution.py:256
  158.5 20.1 %collective-permute-start.34 = (f16[512,512]{1,0:T(8,128)(2,1)S(1)}, f16[512,512]{1,0:T(8,128)(2,1)S(1)}, u32[]{:S(2)}, u32[]{:S(2)}) collective-permute-start(f16[512,512]{1,0:T(8,128)(2,1)S(1)} %collective-permute-done.31), channel_id=1, source_target_pairs={{0,8},{4,12},{8,16},{12,20},{16,24},{20,28},{24,0},{28,4},{1,9},{5... | collective-permute-start | bytes 1572872 | tf_op jit(solution)/shard_map/ppermute | solution.py:252
  178.6 9.0 %collective-permute-start.35 = (f16[256,512]{1,0:T(8,128)(2,1)S(1)}, f16[256,512]{1,0:T(8,128)(2,1)S(1)}, u32[]{:S(2)}, u32[]{:S(2)}) collective-permute-start(f16[256,512]{1,0:T(8,128)(2,1)S(1)} %slice.48), channel_id=1, source_target_pairs={{0,4},{4,0},{8,12},{12,8},{16,20},{20,16},{24,28},{28,24},{1,5},{5... | collective-permute-start | bytes 786440 | tf_op jit(solution)/shard_map/ppermute | solution.py:256
  180.2 11.0 %collective-permute-start.36 = (f16[256,512]{1,0:T(8,128)(2,1)S(1)}, f16[256,512]{1,0:T(8,128)(2,1)S(1)}, u32[]{:S(2)}, u32[]{:S(2)}) collective-permute-start(f16[256,512]{1,0:T(8,128)(2,1)S(1)} %slice.49), channel_id=1, source_target_pairs={{0,8},{4,12},{8,16},{12,20},{16,24},{20,28},{24,0},{28,4},{1,9},{5... | collective-permute-start | bytes 786440 | tf_op jit(solution)/shard_map/ppermute | solution.py:252
